TPU v7x, 32 devices: a 4x4x1 block of a 4x4x8 slice. The times are simulated.
32 devices in a mesh: dp: 1 (over z), sp: 4 (over y), cp: 8 (over x, core).
Axes of the slice: x: 4, y: 4, z: 1, core: 2. Of those that a mesh axis runs over, the one named last changes fastest.
The devices are a block of a 4x4x8 slice.
Arguments:
- x_chunk: bfloat16 [4096, 5120], P(('dp', 'sp', 'cp'))
- k_cache: bfloat16 [4096, 40, 128], P(('dp', 'sp', 'cp'))
- v_cache: bfloat16 [4096, 40, 128], P(('dp', 'sp', 'cp'))
- w_q: bfloat16 [5120, 5120], replicated
- w_k: bfloat16 [5120, 5120], replicated
- w_v: bfloat16 [5120, 5120], replicated
- w_o: bfloat16 [5120, 5120], replicated
Outputs:
- output 1: bfloat16 [4096, 5120], P(('dp', 'sp', 'cp'))
- output 2: bfloat16 [4096, 40, 128], P(('dp', 'sp', 'cp'))
- output 3: bfloat16 [4096, 40, 128], P(('dp', 'sp', 'cp'))
All inputs are finite; a program needn't handle non-finite values.
Results may differ from a plain program's by a relative error of at most 0.00540798.
Values are sent between devices in bfloat16 or wider.
A program may use at most 768 MiB of HBM per device.

v0:
```python
import jax
import jax.numpy as jnp
from jax import lax
from jax.sharding import PartitionSpec as P

ROPE_BASE = 500000
SEQ_AXES = ('sp', 'cp')


def rope_tables(positions, head_dim):
    inv_freq = 1.0 / (ROPE_BASE ** (jnp.arange(0, head_dim, 2, dtype=jnp.float32) / head_dim))
    angles = positions.astype(jnp.float32)[:, None] * inv_freq[None, :]
    return jnp.cos(angles), jnp.sin(angles)


def apply_rope(values, cos_t, sin_t):
    half_dim = values.shape[-1] // 2
    lo_half = values[..., :half_dim].astype(jnp.float32)
    hi_half = values[..., half_dim:].astype(jnp.float32)
    return jnp.concatenate([lo_half * cos_t - hi_half * sin_t, hi_half * cos_t + lo_half * sin_t], axis=-1).astype(jnp.bfloat16)


def attend_block(q_grp, keys, values, attn_scale, allowed=None):
    scores = jnp.einsum('qhgd,khd->hgqk', q_grp, keys, preferred_element_type=jnp.float32) * attn_scale
    if allowed is not None:
        scores = jnp.where(allowed, scores, -jnp.inf)
    row_max = jnp.max(scores, axis=-1)
    exp_scores = jnp.exp(scores - row_max[..., None])
    row_sum = jnp.sum(exp_scores, axis=-1)
    out_part = jnp.einsum('hgqk,khd->hgqd', exp_scores.astype(jnp.bfloat16), values, preferred_element_type=jnp.float32) / row_sum[..., None]
    return out_part, row_max + jnp.log(row_sum)


def merge_parts(out_a, lse_a, out_b, lse_b):
    lse_new = jnp.logaddexp(lse_a, lse_b)
    return out_a * jnp.exp(lse_a - lse_new)[..., None] + out_b * jnp.exp(lse_b - lse_new)[..., None], lse_new


def project_rows(x_loc, w_q, w_k, w_v, kv_heads, head_dim, positions):
    tok_loc = x_loc.shape[0]
    group_size = w_q.shape[1] // (kv_heads * head_dim)
    cos_t, sin_t = rope_tables(positions, head_dim)
    q_rows = jnp.dot(x_loc, w_q, preferred_element_type=jnp.float32).astype(jnp.bfloat16)
    q_grp = apply_rope(q_rows.reshape(tok_loc, kv_heads, group_size, head_dim), cos_t[:, None, None, :], sin_t[:, None, None, :])
    k_rows = jnp.dot(x_loc, w_k, preferred_element_type=jnp.float32).astype(jnp.bfloat16)
    k_new = apply_rope(k_rows.reshape(tok_loc, kv_heads, head_dim), cos_t[:, None, :], sin_t[:, None, :])
    v_new = jnp.dot(x_loc, w_v, preferred_element_type=jnp.float32).astype(jnp.bfloat16).reshape(tok_loc, kv_heads, head_dim)
    return q_grp, k_new, v_new


def solution(mesh):
    seq_size = mesh.shape['sp'] * mesh.shape['cp']
    cp_size = mesh.shape['cp']
    perm_next = [(src_idx, (src_idx + 1) % seq_size) for src_idx in range(seq_size)]
    row_spec = P(('dp', 'sp', 'cp'))

    def local_fn(x_loc, kc_loc, vc_loc, w_q, w_k, w_v, w_o):
        tok_loc, d_model = x_loc.shape
        cache_loc, kv_heads, head_dim = kc_loc.shape
        group_size = w_q.shape[1] // (kv_heads * head_dim)
        attn_scale = head_dim ** -0.5
        seq_idx = lax.axis_index('sp') * cp_size + lax.axis_index('cp')
        q_pos = seq_idx * tok_loc + jnp.arange(tok_loc)
        q_grp, k_new, v_new = project_rows(x_loc, w_q, w_k, w_v, kv_heads, head_dim, cache_loc * seq_size + q_pos)
        diag_mask = jnp.arange(tok_loc)[None, :] <= jnp.arange(tok_loc)[:, None]
        acc_out, acc_lse = attend_block(q_grp, k_new, v_new, attn_scale, diag_mask)
        k_fresh = lax.all_gather(k_new, SEQ_AXES, axis=0, tiled=True)
        v_fresh = lax.all_gather(v_new, SEQ_AXES, axis=0, tiled=True)

        def earlier_step(blk_idx, acc_state):
            k_blk = lax.dynamic_slice_in_dim(k_fresh, blk_idx * tok_loc, tok_loc, axis=0)
            v_blk = lax.dynamic_slice_in_dim(v_fresh, blk_idx * tok_loc, tok_loc, axis=0)
            out_part, lse_part = attend_block(q_grp, k_blk, v_blk, attn_scale)
            return merge_parts(acc_state[0], acc_state[1], out_part, lse_part)

        acc_out, acc_lse = lax.fori_loop(0, seq_idx, earlier_step, (acc_out, acc_lse))
        out_part, lse_part = attend_block(q_grp, kc_loc, vc_loc, attn_scale)
        acc_out, acc_lse = merge_parts(acc_out, acc_lse, out_part, lse_part)

        def cache_step(step_idx, loop_state):
            k_blk, v_blk, acc_o, acc_l = loop_state
            k_blk = lax.ppermute(k_blk, SEQ_AXES, perm_next)
            v_blk = lax.ppermute(v_blk, SEQ_AXES, perm_next)
            part_o, part_l = attend_block(q_grp, k_blk, v_blk, attn_scale)
            acc_o, acc_l = merge_parts(acc_o, acc_l, part_o, part_l)
            return k_blk, v_blk, acc_o, acc_l

        loop_state = lax.fori_loop(1, seq_size, cache_step, (kc_loc, vc_loc, acc_out, acc_lse))
        attn_bf = loop_state[2].astype(jnp.bfloat16)
        w_heads = w_o.reshape(kv_heads, group_size, head_dim, d_model)
        y_loc = jnp.einsum('hgqd,hgdm->qm', attn_bf, w_heads, preferred_element_type=jnp.float32).astype(jnp.bfloat16)
        return y_loc, k_new, v_new

    return jax.shard_map(local_fn, mesh=mesh, in_specs=(row_spec, row_spec, row_spec, P(), P(), P(), P()), out_specs=(row_spec, row_spec, row_spec), check_vma=False)
```

profile of v0, /device:TPU:97, one launch (start us, length us, event | category | flops | bytes accessed | tf_op | source)
XLA Modules:
  0.0 1968.6 jit_solution(8177625890496028536)
XLA Ops:
  8.5 18.2 fusion.46
  30.8 18.2 convolution_convert_fusion
  53.4 18.2 fusion.47
  88.4 77.0 %all-gather.3.cloned.1.call-done = bf16[4096,40,128]{2,0,1:T(8,128)(2,1)} async-done(((bf16[128,40,128]{2,0,1:T(8,128)(2,1)}), bf16[4096,40,128]{2,0,1:T(8,128)(2,1)}) %all-gather.3.cloned.1.call-update) | async-done | bytes 41943056 | tf_op jit(solution)/shard_map/all_gather | solution.py:67
  165.4 132.2 %all-gather.5.cloned.1.call-done = bf16[4096,40,128]{2,1,0:T(8,128)(2,1)} async-done(((bf16[128,40,128]{2,1,0:T(8,128)(2,1)}), bf16[4096,40,128]{2,1,0:T(8,128)(2,1)}) %all-gather.5.cloned.1.call-update) | async-done | bytes 41943056 | tf_op jit(solution)/shard_map/all_gather | solution.py:68
  297.6 10.6 while.28
  301.9 6.2 bitcast_add_fusion.8
  308.2 7.0 bitcast_add_fusion.4
  315.2 1625.9 %while.29 = (s32[]{:T(128)}, bf16[128,40,128]{2,0,1:T(8,128)(2,1)}, bf16[128,40,128]{2,0,1:T(8,128)(2,1)}, f32[40,1,128,128]{3,2,0,1:T(8,128)}, f32[40,1,128]{2,...) while((s32[]{:T(128)}, bf16[128,40,128]{2,0,1:T(8,128)(2,1)}, ...), condition=%wide.region_11.12_spmd, body=%wide.region_8.11_spmd.sunk | while | flops 343459840 | bytes 54067412 | solution.py:88
  315.2 11.9 collective-permute-start
  327.1 10.8 collective-permute-start.1
  344.3 11.3 collective-permute-done.1
  358.2 4.8 bitcast_add_fusion.9
  367.0 20.2 %collective-permute-start.1 = (bf16[128,40,128]{2,0,1:T(8,128)(2,1)}, bf16[128,40,128]{2,0,1:T(8,128)(2,1)}, u32[]{:S(2)}, u32[]{:S(2)}) collective-permute-start(bf16[128,40,128]{2,0,1:T(8,128)(2,1)} %get-tuple-element.298), channel_id=1, source_target_pairs={{0,1},{1,2},{2,3},{3,4},{4,5},{5,6},{6,7},{7,8},{8,9},{9,10},{10,1... | collective-permute-start | bytes 3932168 | tf_op jit(solution)/shard_map/while/body/eval_jaxpr/ppermute | solution.py:83
  387.2 288.2 %collective-permute-done = bf16[128,40,128]{2,0,1:T(8,128)(2,1)S(1)} collective-permute-done((bf16[128,40,128]{2,0,1:T(8,128)(2,1)}, bf16[128,40,128]{2,0,1:T(8,128)(2,1)S(1)}, u32[]{:S(2)}, u32[]{:S(2)}) %collective-permute-start) | collective-permute-done | bytes 1310752 | tf_op jit(solution)/shard_map/while/body/eval_jaxpr/ppermute | solution.py:82
  687.1 31.5 %collective-permute-done = bf16[128,40,128]{2,0,1:T(8,128)(2,1)S(1)} collective-permute-done((bf16[128,40,128]{2,0,1:T(8,128)(2,1)}, bf16[128,40,128]{2,0,1:T(8,128)(2,1)S(1)}, u32[]{:S(2)}, u32[]{:S(2)}) %collective-permute-start) | collective-permute-done | bytes 1310752 | tf_op jit(solution)/shard_map/while/body/eval_jaxpr/ppermute | solution.py:82
  730.3 31.5 %collective-permute-done = bf16[128,40,128]{2,0,1:T(8,128)(2,1)S(1)} collective-permute-done((bf16[128,40,128]{2,0,1:T(8,128)(2,1)}, bf16[128,40,128]{2,0,1:T(8,128)(2,1)S(1)}, u32[]{:S(2)}, u32[]{:S(2)}) %collective-permute-start) | collective-permute-done | bytes 1310752 | tf_op jit(solution)/shard_map/while/body/eval_jaxpr/ppermute | solution.py:82
  767.3 4.8 bitcast_add_fusion.9
  773.6 31.5 %collective-permute-done = bf16[128,40,128]{2,0,1:T(8,128)(2,1)S(1)} collective-permute-done((bf16[128,40,128]{2,0,1:T(8,128)(2,1)}, bf16[128,40,128]{2,0,1:T(8,128)(2,1)S(1)}, u32[]{:S(2)}, u32[]{:S(2)}) %collective-permute-start) | collective-permute-done | bytes 1310752 | tf_op jit(solution)/shard_map/while/body/eval_jaxpr/ppermute | solution.py:82
  810.5 4.8 bitcast_add_fusion.9
  816.8 31.5 %collective-permute-done = bf16[128,40,128]{2,0,1:T(8,128)(2,1)S(1)} collective-permute-done((bf16[128,40,128]{2,0,1:T(8,128)(2,1)}, bf16[128,40,128]{2,0,1:T(8,128)(2,1)S(1)}, u32[]{:S(2)}, u32[]{:S(2)}) %collective-permute-start) | collective-permute-done | bytes 1310752 | tf_op jit(solution)/shard_map/while/body/eval_jaxpr/ppermute | solution.py:82
  860.0 31.5 %collective-permute-done = bf16[128,40,128]{2,0,1:T(8,128)(2,1)S(1)} collective-permute-done((bf16[128,40,128]{2,0,1:T(8,128)(2,1)}, bf16[128,40,128]{2,0,1:T(8,128)(2,1)S(1)}, u32[]{:S(2)}, u32[]{:S(2)}) %collective-permute-start) | collective-permute-done | bytes 1310752 | tf_op jit(solution)/shard_map/while/body/eval_jaxpr/ppermute | solution.py:82
  903.3 31.5 %collective-permute-done = bf16[128,40,128]{2,0,1:T(8,128)(2,1)S(1)} collective-permute-done((bf16[128,40,128]{2,0,1:T(8,128)(2,1)}, bf16[128,40,128]{2,0,1:T(8,128)(2,1)S(1)}, u32[]{:S(2)}, u32[]{:S(2)}) %collective-permute-start) | collective-permute-done | bytes 1310752 | tf_op jit(solution)/shard_map/while/body/eval_jaxpr/ppermute | solution.py:82
  940.2 4.8 bitcast_add_fusion.9
  946.5 31.5 %collective-permute-done = bf16[128,40,128]{2,0,1:T(8,128)(2,1)S(1)} collective-permute-done((bf16[128,40,128]{2,0,1:T(8,128)(2,1)}, bf16[128,40,128]{2,0,1:T(8,128)(2,1)S(1)}, u32[]{:S(2)}, u32[]{:S(2)}) %collective-permute-start) | collective-permute-done | bytes 1310752 | tf_op jit(solution)/shard_map/while/body/eval_jaxpr/ppermute | solution.py:82
  989.8 31.5 %collective-permute-done = bf16[128,40,128]{2,0,1:T(8,128)(2,1)S(1)} collective-permute-done((bf16[128,40,128]{2,0,1:T(8,128)(2,1)}, bf16[128,40,128]{2,0,1:T(8,128)(2,1)S(1)}, u32[]{:S(2)}, u32[]{:S(2)}) %collective-permute-start) | collective-permute-done | bytes 1310752 | tf_op jit(solution)/shard_map/while/body/eval_jaxpr/ppermute | solution.py:82
  1033.0 31.5 %collective-permute-done = bf16[128,40,128]{2,0,1:T(8,128)(2,1)S(1)} collective-permute-done((bf16[128,40,128]{2,0,1:T(8,128)(2,1)}, bf16[128,40,128]{2,0,1:T(8,128)(2,1)S(1)}, u32[]{:S(2)}, u32[]{:S(2)}) %collective-permute-start) | collective-permute-done | bytes 1310752 | tf_op jit(solution)/shard_map/while/body/eval_jaxpr/ppermute | solution.py:82
  1076.3 31.5 %collective-permute-done = bf16[128,40,128]{2,0,1:T(8,128)(2,1)S(1)} collective-permute-done((bf16[128,40,128]{2,0,1:T(8,128)(2,1)}, bf16[128,40,128]{2,0,1:T(8,128)(2,1)S(1)}, u32[]{:S(2)}, u32[]{:S(2)}) %collective-permute-start) | collective-permute-done | bytes 1310752 | tf_op jit(solution)/shard_map/while/body/eval_jaxpr/ppermute | solution.py:82
  1119.5 31.5 %collective-permute-done = bf16[128,40,128]{2,0,1:T(8,128)(2,1)S(1)} collective-permute-done((bf16[128,40,128]{2,0,1:T(8,128)(2,1)}, bf16[128,40,128]{2,0,1:T(8,128)(2,1)S(1)}, u32[]{:S(2)}, u32[]{:S(2)}) %collective-permute-start) | collective-permute-done | bytes 1310752 | tf_op jit(solution)/shard_map/while/body/eval_jaxpr/ppermute | solution.py:82
  1162.7 31.5 %collective-permute-done = bf16[128,40,128]{2,0,1:T(8,128)(2,1)S(1)} collective-permute-done((bf16[128,40,128]{2,0,1:T(8,128)(2,1)}, bf16[128,40,128]{2,0,1:T(8,128)(2,1)S(1)}, u32[]{:S(2)}, u32[]{:S(2)}) %collective-permute-start) | collective-permute-done | bytes 1310752 | tf_op jit(solution)/shard_map/while/body/eval_jaxpr/ppermute | solution.py:82
  1206.0 31.5 %collective-permute-done = bf16[128,40,128]{2,0,1:T(8,128)(2,1)S(1)} collective-permute-done((bf16[128,40,128]{2,0,1:T(8,128)(2,1)}, bf16[128,40,128]{2,0,1:T(8,128)(2,1)S(1)}, u32[]{:S(2)}, u32[]{:S(2)}) %collective-permute-start) | collective-permute-done | bytes 1310752 | tf_op jit(solution)/shard_map/while/body/eval_jaxpr/ppermute | solution.py:82
  1249.2 31.5 %collective-permute-done = bf16[128,40,128]{2,0,1:T(8,128)(2,1)S(1)} collective-permute-done((bf16[128,40,128]{2,0,1:T(8,128)(2,1)}, bf16[128,40,128]{2,0,1:T(8,128)(2,1)S(1)}, u32[]{:S(2)}, u32[]{:S(2)}) %collective-permute-start) | collective-permute-done | bytes 1310752 | tf_op jit(solution)/shard_map/while/body/eval_jaxpr/ppermute | solution.py:82
  1292.5 31.5 %collective-permute-done = bf16[128,40,128]{2,0,1:T(8,128)(2,1)S(1)} collective-permute-done((bf16[128,40,128]{2,0,1:T(8,128)(2,1)}, bf16[128,40,128]{2,0,1:T(8,128)(2,1)S(1)}, u32[]{:S(2)}, u32[]{:S(2)}) %collective-permute-start) | collective-permute-done | bytes 1310752 | tf_op jit(solution)/shard_map/while/body/eval_jaxpr/ppermute | solution.py:82
  1335.7 31.5 %collective-permute-done = bf16[128,40,128]{2,0,1:T(8,128)(2,1)S(1)} collective-permute-done((bf16[128,40,128]{2,0,1:T(8,128)(2,1)}, bf16[128,40,128]{2,0,1:T(8,128)(2,1)S(1)}, u32[]{:S(2)}, u32[]{:S(2)}) %collective-permute-start) | collective-permute-done | bytes 1310752 | tf_op jit(solution)/shard_map/while/body/eval_jaxpr/ppermute | solution.py:82
  1379.0 31.5 %collective-permute-done = bf16[128,40,128]{2,0,1:T(8,128)(2,1)S(1)} collective-permute-done((bf16[128,40,128]{2,0,1:T(8,128)(2,1)}, bf16[128,40,128]{2,0,1:T(8,128)(2,1)S(1)}, u32[]{:S(2)}, u32[]{:S(2)}) %collective-permute-start) | collective-permute-done | bytes 1310752 | tf_op jit(solution)/shard_map/while/body/eval_jaxpr/ppermute | solution.py:82
  1422.2 31.5 %collective-permute-done = bf16[128,40,128]{2,0,1:T(8,128)(2,1)S(1)} collective-permute-done((bf16[128,40,128]{2,0,1:T(8,128)(2,1)}, bf16[128,40,128]{2,0,1:T(8,128)(2,1)S(1)}, u32[]{:S(2)}, u32[]{:S(2)}) %collective-permute-start) | collective-permute-done | bytes 1310752 | tf_op jit(solution)/shard_map/while/body/eval_jaxpr/ppermute | solution.py:82
  1465.4 31.5 %collective-permute-done = bf16[128,40,128]{2,0,1:T(8,128)(2,1)S(1)} collective-permute-done((bf16[128,40,128]{2,0,1:T(8,128)(2,1)}, bf16[128,40,128]{2,0,1:T(8,128)(2,1)S(1)}, u32[]{:S(2)}, u32[]{:S(2)}) %collective-permute-start) | collective-permute-done | bytes 1310752 | tf_op jit(solution)/shard_map/while/body/eval_jaxpr/ppermute | solution.py:82
  1508.7 31.5 %collective-permute-done = bf16[128,40,128]{2,0,1:T(8,128)(2,1)S(1)} collective-permute-done((bf16[128,40,128]{2,0,1:T(8,128)(2,1)}, bf16[128,40,128]{2,0,1:T(8,128)(2,1)S(1)}, u32[]{:S(2)}, u32[]{:S(2)}) %collective-permute-start) | collective-permute-done | bytes 1310752 | tf_op jit(solution)/shard_map/while/body/eval_jaxpr/ppermute | solution.py:82
  1551.9 31.5 %collective-permute-done = bf16[128,40,128]{2,0,1:T(8,128)(2,1)S(1)} collective-permute-done((bf16[128,40,128]{2,0,1:T(8,128)(2,1)}, bf16[128,40,128]{2,0,1:T(8,128)(2,1)S(1)}, u32[]{:S(2)}, u32[]{:S(2)}) %collective-permute-start) | collective-permute-done | bytes 1310752 | tf_op jit(solution)/shard_map/while/body/eval_jaxpr/ppermute | solution.py:82
  1595.2 31.5 %collective-permute-done = bf16[128,40,128]{2,0,1:T(8,128)(2,1)S(1)} collective-permute-done((bf16[128,40,128]{2,0,1:T(8,128)(2,1)}, bf16[128,40,128]{2,0,1:T(8,128)(2,1)S(1)}, u32[]{:S(2)}, u32[]{:S(2)}) %collective-permute-start) | collective-permute-done | bytes 1310752 | tf_op jit(solution)/shard_map/while/body/eval_jaxpr/ppermute | solution.py:82
  1638.4 31.5 %collective-permute-done = bf16[128,40,128]{2,0,1:T(8,128)(2,1)S(1)} collective-permute-done((bf16[128,40,128]{2,0,1:T(8,128)(2,1)}, bf16[128,40,128]{2,0,1:T(8,128)(2,1)S(1)}, u32[]{:S(2)}, u32[]{:S(2)}) %collective-permute-start) | collective-permute-done | bytes 1310752 | tf_op jit(solution)/shard_map/while/body/eval_jaxpr/ppermute | solution.py:82
  1681.6 31.5 %collective-permute-done = bf16[128,40,128]{2,0,1:T(8,128)(2,1)S(1)} collective-permute-done((bf16[128,40,128]{2,0,1:T(8,128)(2,1)}, bf16[128,40,128]{2,0,1:T(8,128)(2,1)S(1)}, u32[]{:S(2)}, u32[]{:S(2)}) %collective-permute-start) | collective-permute-done | bytes 1310752 | tf_op jit(solution)/shard_map/while/body/eval_jaxpr/ppermute | solution.py:82
  1724.9 31.5 %collective-permute-done = bf16[128,40,128]{2,0,1:T(8,128)(2,1)S(1)} collective-permute-done((bf16[128,40,128]{2,0,1:T(8,128)(2,1)}, bf16[128,40,128]{2,0,1:T(8,128)(2,1)S(1)}, u32[]{:S(2)}, u32[]{:S(2)}) %collective-permute-start) | collective-permute-done | bytes 1310752 | tf_op jit(solution)/shard_map/while/body/eval_jaxpr/ppermute | solution.py:82
  1768.1 31.5 %collective-permute-done = bf16[128,40,128]{2,0,1:T(8,128)(2,1)S(1)} collective-permute-done((bf16[128,40,128]{2,0,1:T(8,128)(2,1)}, bf16[128,40,128]{2,0,1:T(8,128)(2,1)S(1)}, u32[]{:S(2)}, u32[]{:S(2)}) %collective-permute-start) | collective-permute-done | bytes 1310752 | tf_op jit(solution)/shard_map/while/body/eval_jaxpr/ppermute | solution.py:82
  1811.4 31.5 %collective-permute-done = bf16[128,40,128]{2,0,1:T(8,128)(2,1)S(1)} collective-permute-done((bf16[128,40,128]{2,0,1:T(8,128)(2,1)}, bf16[128,40,128]{2,0,1:T(8,128)(2,1)S(1)}, u32[]{:S(2)}, u32[]{:S(2)}) %collective-permute-start) | collective-permute-done | bytes 1310752 | tf_op jit(solution)/shard_map/while/body/eval_jaxpr/ppermute | solution.py:82
  1854.6 31.5 %collective-permute-done = bf16[128,40,128]{2,0,1:T(8,128)(2,1)S(1)} collective-permute-done((bf16[128,40,128]{2,0,1:T(8,128)(2,1)}, bf16[128,40,128]{2,0,1:T(8,128)(2,1)S(1)}, u32[]{:S(2)}, u32[]{:S(2)}) %collective-permute-start) | collective-permute-done | bytes 1310752 | tf_op jit(solution)/shard_map/while/body/eval_jaxpr/ppermute | solution.py:82
  1897.9 31.5 %collective-permute-done = bf16[128,40,128]{2,0,1:T(8,128)(2,1)S(1)} collective-permute-done((bf16[128,40,128]{2,0,1:T(8,128)(2,1)}, bf16[128,40,128]{2,0,1:T(8,128)(2,1)S(1)}, u32[]{:S(2)}, u32[]{:S(2)}) %collective-permute-start) | collective-permute-done | bytes 1310752 | tf_op jit(solution)/shard_map/while/body/eval_jaxpr/ppermute | solution.py:82
  1941.1 20.7 %fusion.31 = bf16[128,5120]{1,0:T(8,128)(2,1)} fusion(bf16[40,128,5120]{2,1,0:T(8,128)(2,1)} %bitcast.232, f32[40,1,128,128]{3,2,0,1:T(8,128)} %get-tuple-element.76), kind=kOutput, calls=%fused_computation.49 | convolution fusion | flops 6712197120 | bytes 56360960 | tf_op jit(solution)/shard_map/hgqd,hgdm->qm/dot_general | solution.py:91
  (476 shorter events, 379.7 us)
Async XLA Ops:
  7.2 158.2 %all-gather.3.cloned.1.call-start = ((), (), s32[]{:S(2)}) async-start(), calls=%async_computation | async-start | bytes 43253760 | tf_op jit(solution)/shard_map/all_gather | solution.py:67
  30.6 267.0 %all-gather.5.cloned.1.call-start = ((), (), s32[]{:S(2)}) async-start(), calls=%async_computation.1 | async-start | bytes 43253760 | tf_op jit(solution)/shard_map/all_gather | solution.py:68
  364.5 310.9 %collective-permute-start = (bf16[128,40,128]{2,0,1:T(8,128)(2,1)}, bf16[128,40,128]{2,0,1:T(8,128)(2,1)S(1)}, u32[]{:S(2)}, u32[]{:S(2)}) collective-permute-start(bf16[128,40,128]{2,0,1:T(8,128)(2,1)} %get-tuple-element.297), channel_id=1, source_target_pairs={{0,1},{1,2},{2,3},{3,4},{4,5},{5,6},{6,7},{7,8},{8,9},{9,10},{10,1... | collective-permute-start | bytes 3932168 | tf_op jit(solution)/shard_map/while/body/eval_jaxpr/ppermute | solution.py:82
  367.0 311.1 %collective-permute-start.1 = (bf16[128,40,128]{2,0,1:T(8,128)(2,1)}, bf16[128,40,128]{2,0,1:T(8,128)(2,1)}, u32[]{:S(2)}, u32[]{:S(2)}) collective-permute-start(bf16[128,40,128]{2,0,1:T(8,128)(2,1)} %get-tuple-element.298), channel_id=1, source_target_pairs={{0,1},{1,2},{2,3},{3,4},{4,5},{5,6},{6,7},{7,8},{8,9},{9,10},{10,1... | collective-permute-start | bytes 3932168 | tf_op jit(solution)/shard_map/while/body/eval_jaxpr/ppermute | solution.py:83
  687.1 31.5 %collective-permute-start = (bf16[128,40,128]{2,0,1:T(8,128)(2,1)}, bf16[128,40,128]{2,0,1:T(8,128)(2,1)S(1)}, u32[]{:S(2)}, u32[]{:S(2)}) collective-permute-start(bf16[128,40,128]{2,0,1:T(8,128)(2,1)} %get-tuple-element.297), channel_id=1, source_target_pairs={{0,1},{1,2},{2,3},{3,4},{4,5},{5,6},{6,7},{7,8},{8,9},{9,10},{10,1... | collective-permute-start | bytes 3932168 | tf_op jit(solution)/shard_map/while/body/eval_jaxpr/ppermute | solution.py:82
  687.1 34.2 %collective-permute-start.1 = (bf16[128,40,128]{2,0,1:T(8,128)(2,1)}, bf16[128,40,128]{2,0,1:T(8,128)(2,1)}, u32[]{:S(2)}, u32[]{:S(2)}) collective-permute-start(bf16[128,40,128]{2,0,1:T(8,128)(2,1)} %get-tuple-element.298), channel_id=1, source_target_pairs={{0,1},{1,2},{2,3},{3,4},{4,5},{5,6},{6,7},{7,8},{8,9},{9,10},{10,1... | collective-permute-start | bytes 3932168 | tf_op jit(solution)/shard_map/while/body/eval_jaxpr/ppermute | solution.py:83
  730.3 31.5 %collective-permute-start = (bf16[128,40,128]{2,0,1:T(8,128)(2,1)}, bf16[128,40,128]{2,0,1:T(8,128)(2,1)S(1)}, u32[]{:S(2)}, u32[]{:S(2)}) collective-permute-start(bf16[128,40,128]{2,0,1:T(8,128)(2,1)} %get-tuple-element.297), channel_id=1, source_target_pairs={{0,1},{1,2},{2,3},{3,4},{4,5},{5,6},{6,7},{7,8},{8,9},{9,10},{10,1... | collective-permute-start | bytes 3932168 | tf_op jit(solution)/shard_map/while/body/eval_jaxpr/ppermute | solution.py:82
  730.3 34.2 %collective-permute-start.1 = (bf16[128,40,128]{2,0,1:T(8,128)(2,1)}, bf16[128,40,128]{2,0,1:T(8,128)(2,1)}, u32[]{:S(2)}, u32[]{:S(2)}) collective-permute-start(bf16[128,40,128]{2,0,1:T(8,128)(2,1)} %get-tuple-element.298), channel_id=1, source_target_pairs={{0,1},{1,2},{2,3},{3,4},{4,5},{5,6},{6,7},{7,8},{8,9},{9,10},{10,1... | collective-permute-start | bytes 3932168 | tf_op jit(solution)/shard_map/while/body/eval_jaxpr/ppermute | solution.py:83
  773.6 31.5 %collective-permute-start = (bf16[128,40,128]{2,0,1:T(8,128)(2,1)}, bf16[128,40,128]{2,0,1:T(8,128)(2,1)S(1)}, u32[]{:S(2)}, u32[]{:S(2)}) collective-permute-start(bf16[128,40,128]{2,0,1:T(8,128)(2,1)} %get-tuple-element.297), channel_id=1, source_target_pairs={{0,1},{1,2},{2,3},{3,4},{4,5},{5,6},{6,7},{7,8},{8,9},{9,10},{10,1... | collective-permute-start | bytes 3932168 | tf_op jit(solution)/shard_map/while/body/eval_jaxpr/ppermute | solution.py:82
  773.6 34.2 %collective-permute-start.1 = (bf16[128,40,128]{2,0,1:T(8,128)(2,1)}, bf16[128,40,128]{2,0,1:T(8,128)(2,1)}, u32[]{:S(2)}, u32[]{:S(2)}) collective-permute-start(bf16[128,40,128]{2,0,1:T(8,128)(2,1)} %get-tuple-element.298), channel_id=1, source_target_pairs={{0,1},{1,2},{2,3},{3,4},{4,5},{5,6},{6,7},{7,8},{8,9},{9,10},{10,1... | collective-permute-start | bytes 3932168 | tf_op jit(solution)/shard_map/while/body/eval_jaxpr/ppermute | solution.py:83
  816.8 31.5 %collective-permute-start = (bf16[128,40,128]{2,0,1:T(8,128)(2,1)}, bf16[128,40,128]{2,0,1:T(8,128)(2,1)S(1)}, u32[]{:S(2)}, u32[]{:S(2)}) collective-permute-start(bf16[128,40,128]{2,0,1:T(8,128)(2,1)} %get-tuple-element.297), channel_id=1, source_target_pairs={{0,1},{1,2},{2,3},{3,4},{4,5},{5,6},{6,7},{7,8},{8,9},{9,10},{10,1... | collective-permute-start | bytes 3932168 | tf_op jit(solution)/shard_map/while/body/eval_jaxpr/ppermute | solution.py:82
  816.8 34.2 %collective-permute-start.1 = (bf16[128,40,128]{2,0,1:T(8,128)(2,1)}, bf16[128,40,128]{2,0,1:T(8,128)(2,1)}, u32[]{:S(2)}, u32[]{:S(2)}) collective-permute-start(bf16[128,40,128]{2,0,1:T(8,128)(2,1)} %get-tuple-element.298), channel_id=1, source_target_pairs={{0,1},{1,2},{2,3},{3,4},{4,5},{5,6},{6,7},{7,8},{8,9},{9,10},{10,1... | collective-permute-start | bytes 3932168 | tf_op jit(solution)/shard_map/while/body/eval_jaxpr/ppermute | solution.py:83
  860.0 31.5 %collective-permute-start = (bf16[128,40,128]{2,0,1:T(8,128)(2,1)}, bf16[128,40,128]{2,0,1:T(8,128)(2,1)S(1)}, u32[]{:S(2)}, u32[]{:S(2)}) collective-permute-start(bf16[128,40,128]{2,0,1:T(8,128)(2,1)} %get-tuple-element.297), channel_id=1, source_target_pairs={{0,1},{1,2},{2,3},{3,4},{4,5},{5,6},{6,7},{7,8},{8,9},{9,10},{10,1... | collective-permute-start | bytes 3932168 | tf_op jit(solution)/shard_map/while/body/eval_jaxpr/ppermute | solution.py:82
  860.0 34.2 %collective-permute-start.1 = (bf16[128,40,128]{2,0,1:T(8,128)(2,1)}, bf16[128,40,128]{2,0,1:T(8,128)(2,1)}, u32[]{:S(2)}, u32[]{:S(2)}) collective-permute-start(bf16[128,40,128]{2,0,1:T(8,128)(2,1)} %get-tuple-element.298), channel_id=1, source_target_pairs={{0,1},{1,2},{2,3},{3,4},{4,5},{5,6},{6,7},{7,8},{8,9},{9,10},{10,1... | collective-permute-start | bytes 3932168 | tf_op jit(solution)/shard_map/while/body/eval_jaxpr/ppermute | solution.py:83
  903.3 31.5 %collective-permute-start = (bf16[128,40,128]{2,0,1:T(8,128)(2,1)}, bf16[128,40,128]{2,0,1:T(8,128)(2,1)S(1)}, u32[]{:S(2)}, u32[]{:S(2)}) collective-permute-start(bf16[128,40,128]{2,0,1:T(8,128)(2,1)} %get-tuple-element.297), channel_id=1, source_target_pairs={{0,1},{1,2},{2,3},{3,4},{4,5},{5,6},{6,7},{7,8},{8,9},{9,10},{10,1... | collective-permute-start | bytes 3932168 | tf_op jit(solution)/shard_map/while/body/eval_jaxpr/ppermute | solution.py:82
  903.3 34.2 %collective-permute-start.1 = (bf16[128,40,128]{2,0,1:T(8,128)(2,1)}, bf16[128,40,128]{2,0,1:T(8,128)(2,1)}, u32[]{:S(2)}, u32[]{:S(2)}) collective-permute-start(bf16[128,40,128]{2,0,1:T(8,128)(2,1)} %get-tuple-element.298), channel_id=1, source_target_pairs={{0,1},{1,2},{2,3},{3,4},{4,5},{5,6},{6,7},{7,8},{8,9},{9,10},{10,1... | collective-permute-start | bytes 3932168 | tf_op jit(solution)/shard_map/while/body/eval_jaxpr/ppermute | solution.py:83
  946.5 31.5 %collective-permute-start = (bf16[128,40,128]{2,0,1:T(8,128)(2,1)}, bf16[128,40,128]{2,0,1:T(8,128)(2,1)S(1)}, u32[]{:S(2)}, u32[]{:S(2)}) collective-permute-start(bf16[128,40,128]{2,0,1:T(8,128)(2,1)} %get-tuple-element.297), channel_id=1, source_target_pairs={{0,1},{1,2},{2,3},{3,4},{4,5},{5,6},{6,7},{7,8},{8,9},{9,10},{10,1... | collective-permute-start | bytes 3932168 | tf_op jit(solution)/shard_map/while/body/eval_jaxpr/ppermute | solution.py:82
  946.5 34.2 %collective-permute-start.1 = (bf16[128,40,128]{2,0,1:T(8,128)(2,1)}, bf16[128,40,128]{2,0,1:T(8,128)(2,1)}, u32[]{:S(2)}, u32[]{:S(2)}) collective-permute-start(bf16[128,40,128]{2,0,1:T(8,128)(2,1)} %get-tuple-element.298), channel_id=1, source_target_pairs={{0,1},{1,2},{2,3},{3,4},{4,5},{5,6},{6,7},{7,8},{8,9},{9,10},{10,1... | collective-permute-start | bytes 3932168 | tf_op jit(solution)/shard_map/while/body/eval_jaxpr/ppermute | solution.py:83
  989.8 31.5 %collective-permute-start = (bf16[128,40,128]{2,0,1:T(8,128)(2,1)}, bf16[128,40,128]{2,0,1:T(8,128)(2,1)S(1)}, u32[]{:S(2)}, u32[]{:S(2)}) collective-permute-start(bf16[128,40,128]{2,0,1:T(8,128)(2,1)} %get-tuple-element.297), channel_id=1, source_target_pairs={{0,1},{1,2},{2,3},{3,4},{4,5},{5,6},{6,7},{7,8},{8,9},{9,10},{10,1... | collective-permute-start | bytes 3932168 | tf_op jit(solution)/shard_map/while/body/eval_jaxpr/ppermute | solution.py:82
  989.8 34.2 %collective-permute-start.1 = (bf16[128,40,128]{2,0,1:T(8,128)(2,1)}, bf16[128,40,128]{2,0,1:T(8,128)(2,1)}, u32[]{:S(2)}, u32[]{:S(2)}) collective-permute-start(bf16[128,40,128]{2,0,1:T(8,128)(2,1)} %get-tuple-element.298), channel_id=1, source_target_pairs={{0,1},{1,2},{2,3},{3,4},{4,5},{5,6},{6,7},{7,8},{8,9},{9,10},{10,1... | collective-permute-start | bytes 3932168 | tf_op jit(solution)/shard_map/while/body/eval_jaxpr/ppermute | solution.py:83
  1033.0 31.5 %collective-permute-start = (bf16[128,40,128]{2,0,1:T(8,128)(2,1)}, bf16[128,40,128]{2,0,1:T(8,128)(2,1)S(1)}, u32[]{:S(2)}, u32[]{:S(2)}) collective-permute-start(bf16[128,40,128]{2,0,1:T(8,128)(2,1)} %get-tuple-element.297), channel_id=1, source_target_pairs={{0,1},{1,2},{2,3},{3,4},{4,5},{5,6},{6,7},{7,8},{8,9},{9,10},{10,1... | collective-permute-start | bytes 3932168 | tf_op jit(solution)/shard_map/while/body/eval_jaxpr/ppermute | solution.py:82
  1033.0 34.2 %collective-permute-start.1 = (bf16[128,40,128]{2,0,1:T(8,128)(2,1)}, bf16[128,40,128]{2,0,1:T(8,128)(2,1)}, u32[]{:S(2)}, u32[]{:S(2)}) collective-permute-start(bf16[128,40,128]{2,0,1:T(8,128)(2,1)} %get-tuple-element.298), channel_id=1, source_target_pairs={{0,1},{1,2},{2,3},{3,4},{4,5},{5,6},{6,7},{7,8},{8,9},{9,10},{10,1... | collective-permute-start | bytes 3932168 | tf_op jit(solution)/shard_map/while/body/eval_jaxpr/ppermute | solution.py:83
  1076.2 31.5 %collective-permute-start = (bf16[128,40,128]{2,0,1:T(8,128)(2,1)}, bf16[128,40,128]{2,0,1:T(8,128)(2,1)S(1)}, u32[]{:S(2)}, u32[]{:S(2)}) collective-permute-start(bf16[128,40,128]{2,0,1:T(8,128)(2,1)} %get-tuple-element.297), channel_id=1, source_target_pairs={{0,1},{1,2},{2,3},{3,4},{4,5},{5,6},{6,7},{7,8},{8,9},{9,10},{10,1... | collective-permute-start | bytes 3932168 | tf_op jit(solution)/shard_map/while/body/eval_jaxpr/ppermute | solution.py:82
  1076.3 34.2 %collective-permute-start.1 = (bf16[128,40,128]{2,0,1:T(8,128)(2,1)}, bf16[128,40,128]{2,0,1:T(8,128)(2,1)}, u32[]{:S(2)}, u32[]{:S(2)}) collective-permute-start(bf16[128,40,128]{2,0,1:T(8,128)(2,1)} %get-tuple-element.298), channel_id=1, source_target_pairs={{0,1},{1,2},{2,3},{3,4},{4,5},{5,6},{6,7},{7,8},{8,9},{9,10},{10,1... | collective-permute-start | bytes 3932168 | tf_op jit(solution)/shard_map/while/body/eval_jaxpr/ppermute | solution.py:83
  1119.5 31.5 %collective-permute-start = (bf16[128,40,128]{2,0,1:T(8,128)(2,1)}, bf16[128,40,128]{2,0,1:T(8,128)(2,1)S(1)}, u32[]{:S(2)}, u32[]{:S(2)}) collective-permute-start(bf16[128,40,128]{2,0,1:T(8,128)(2,1)} %get-tuple-element.297), channel_id=1, source_target_pairs={{0,1},{1,2},{2,3},{3,4},{4,5},{5,6},{6,7},{7,8},{8,9},{9,10},{10,1... | collective-permute-start | bytes 3932168 | tf_op jit(solution)/shard_map/while/body/eval_jaxpr/ppermute | solution.py:82
  1119.5 34.2 %collective-permute-start.1 = (bf16[128,40,128]{2,0,1:T(8,128)(2,1)}, bf16[128,40,128]{2,0,1:T(8,128)(2,1)}, u32[]{:S(2)}, u32[]{:S(2)}) collective-permute-start(bf16[128,40,128]{2,0,1:T(8,128)(2,1)} %get-tuple-element.298), channel_id=1, source_target_pairs={{0,1},{1,2},{2,3},{3,4},{4,5},{5,6},{6,7},{7,8},{8,9},{9,10},{10,1... | collective-permute-start | bytes 3932168 | tf_op jit(solution)/shard_map/while/body/eval_jaxpr/ppermute | solution.py:83
  1162.7 31.5 %collective-permute-start = (bf16[128,40,128]{2,0,1:T(8,128)(2,1)}, bf16[128,40,128]{2,0,1:T(8,128)(2,1)S(1)}, u32[]{:S(2)}, u32[]{:S(2)}) collective-permute-start(bf16[128,40,128]{2,0,1:T(8,128)(2,1)} %get-tuple-element.297), channel_id=1, source_target_pairs={{0,1},{1,2},{2,3},{3,4},{4,5},{5,6},{6,7},{7,8},{8,9},{9,10},{10,1... | collective-permute-start | bytes 3932168 | tf_op jit(solution)/shard_map/while/body/eval_jaxpr/ppermute | solution.py:82
  1162.7 34.2 %collective-permute-start.1 = (bf16[128,40,128]{2,0,1:T(8,128)(2,1)}, bf16[128,40,128]{2,0,1:T(8,128)(2,1)}, u32[]{:S(2)}, u32[]{:S(2)}) collective-permute-start(bf16[128,40,128]{2,0,1:T(8,128)(2,1)} %get-tuple-element.298), channel_id=1, source_target_pairs={{0,1},{1,2},{2,3},{3,4},{4,5},{5,6},{6,7},{7,8},{8,9},{9,10},{10,1... | collective-permute-start | bytes 3932168 | tf_op jit(solution)/shard_map/while/body/eval_jaxpr/ppermute | solution.py:83
  1206.0 31.5 %collective-permute-start = (bf16[128,40,128]{2,0,1:T(8,128)(2,1)}, bf16[128,40,128]{2,0,1:T(8,128)(2,1)S(1)}, u32[]{:S(2)}, u32[]{:S(2)}) collective-permute-start(bf16[128,40,128]{2,0,1:T(8,128)(2,1)} %get-tuple-element.297), channel_id=1, source_target_pairs={{0,1},{1,2},{2,3},{3,4},{4,5},{5,6},{6,7},{7,8},{8,9},{9,10},{10,1... | collective-permute-start | bytes 3932168 | tf_op jit(solution)/shard_map/while/body/eval_jaxpr/ppermute | solution.py:82
  1206.0 34.2 %collective-permute-start.1 = (bf16[128,40,128]{2,0,1:T(8,128)(2,1)}, bf16[128,40,128]{2,0,1:T(8,128)(2,1)}, u32[]{:S(2)}, u32[]{:S(2)}) collective-permute-start(bf16[128,40,128]{2,0,1:T(8,128)(2,1)} %get-tuple-element.298), channel_id=1, source_target_pairs={{0,1},{1,2},{2,3},{3,4},{4,5},{5,6},{6,7},{7,8},{8,9},{9,10},{10,1... | collective-permute-start | bytes 3932168 | tf_op jit(solution)/shard_map/while/body/eval_jaxpr/ppermute | solution.py:83
  1249.2 34.2 %collective-permute-start.1 = (bf16[128,40,128]{2,0,1:T(8,128)(2,1)}, bf16[128,40,128]{2,0,1:T(8,128)(2,1)}, u32[]{:S(2)}, u32[]{:S(2)}) collective-permute-start(bf16[128,40,128]{2,0,1:T(8,128)(2,1)} %get-tuple-element.298), channel_id=1, source_target_pairs={{0,1},{1,2},{2,3},{3,4},{4,5},{5,6},{6,7},{7,8},{8,9},{9,10},{10,1... | collective-permute-start | bytes 3932168 | tf_op jit(solution)/shard_map/while/body/eval_jaxpr/ppermute | solution.py:83
  1292.5 34.2 %collective-permute-start.1 = (bf16[128,40,128]{2,0,1:T(8,128)(2,1)}, bf16[128,40,128]{2,0,1:T(8,128)(2,1)}, u32[]{:S(2)}, u32[]{:S(2)}) collective-permute-start(bf16[128,40,128]{2,0,1:T(8,128)(2,1)} %get-tuple-element.298), channel_id=1, source_target_pairs={{0,1},{1,2},{2,3},{3,4},{4,5},{5,6},{6,7},{7,8},{8,9},{9,10},{10,1... | collective-permute-start | bytes 3932168 | tf_op jit(solution)/shard_map/while/body/eval_jaxpr/ppermute | solution.py:83
  1335.7 34.2 %collective-permute-start.1 = (bf16[128,40,128]{2,0,1:T(8,128)(2,1)}, bf16[128,40,128]{2,0,1:T(8,128)(2,1)}, u32[]{:S(2)}, u32[]{:S(2)}) collective-permute-start(bf16[128,40,128]{2,0,1:T(8,128)(2,1)} %get-tuple-element.298), channel_id=1, source_target_pairs={{0,1},{1,2},{2,3},{3,4},{4,5},{5,6},{6,7},{7,8},{8,9},{9,10},{10,1... | collective-permute-start | bytes 3932168 | tf_op jit(solution)/shard_map/while/body/eval_jaxpr/ppermute | solution.py:83
  1378.9 34.2 %collective-permute-start.1 = (bf16[128,40,128]{2,0,1:T(8,128)(2,1)}, bf16[128,40,128]{2,0,1:T(8,128)(2,1)}, u32[]{:S(2)}, u32[]{:S(2)}) collective-permute-start(bf16[128,40,128]{2,0,1:T(8,128)(2,1)} %get-tuple-element.298), channel_id=1, source_target_pairs={{0,1},{1,2},{2,3},{3,4},{4,5},{5,6},{6,7},{7,8},{8,9},{9,10},{10,1... | collective-permute-start | bytes 3932168 | tf_op jit(solution)/shard_map/while/body/eval_jaxpr/ppermute | solution.py:83
  1422.2 34.2 %collective-permute-start.1 = (bf16[128,40,128]{2,0,1:T(8,128)(2,1)}, bf16[128,40,128]{2,0,1:T(8,128)(2,1)}, u32[]{:S(2)}, u32[]{:S(2)}) collective-permute-start(bf16[128,40,128]{2,0,1:T(8,128)(2,1)} %get-tuple-element.298), channel_id=1, source_target_pairs={{0,1},{1,2},{2,3},{3,4},{4,5},{5,6},{6,7},{7,8},{8,9},{9,10},{10,1... | collective-permute-start | bytes 3932168 | tf_op jit(solution)/shard_map/while/body/eval_jaxpr/ppermute | solution.py:83
  1465.4 34.2 %collective-permute-start.1 = (bf16[128,40,128]{2,0,1:T(8,128)(2,1)}, bf16[128,40,128]{2,0,1:T(8,128)(2,1)}, u32[]{:S(2)}, u32[]{:S(2)}) collective-permute-start(bf16[128,40,128]{2,0,1:T(8,128)(2,1)} %get-tuple-element.298), channel_id=1, source_target_pairs={{0,1},{1,2},{2,3},{3,4},{4,5},{5,6},{6,7},{7,8},{8,9},{9,10},{10,1... | collective-permute-start | bytes 3932168 | tf_op jit(solution)/shard_map/while/body/eval_jaxpr/ppermute | solution.py:83
  1508.7 34.2 %collective-permute-start.1 = (bf16[128,40,128]{2,0,1:T(8,128)(2,1)}, bf16[128,40,128]{2,0,1:T(8,128)(2,1)}, u32[]{:S(2)}, u32[]{:S(2)}) collective-permute-start(bf16[128,40,128]{2,0,1:T(8,128)(2,1)} %get-tuple-element.298), channel_id=1, source_target_pairs={{0,1},{1,2},{2,3},{3,4},{4,5},{5,6},{6,7},{7,8},{8,9},{9,10},{10,1... | collective-permute-start | bytes 3932168 | tf_op jit(solution)/shard_map/while/body/eval_jaxpr/ppermute | solution.py:83
  1551.9 34.2 %collective-permute-start.1 = (bf16[128,40,128]{2,0,1:T(8,128)(2,1)}, bf16[128,40,128]{2,0,1:T(8,128)(2,1)}, u32[]{:S(2)}, u32[]{:S(2)}) collective-permute-start(bf16[128,40,128]{2,0,1:T(8,128)(2,1)} %get-tuple-element.298), channel_id=1, source_target_pairs={{0,1},{1,2},{2,3},{3,4},{4,5},{5,6},{6,7},{7,8},{8,9},{9,10},{10,1... | collective-permute-start | bytes 3932168 | tf_op jit(solution)/shard_map/while/body/eval_jaxpr/ppermute | solution.py:83
  1595.2 34.2 %collective-permute-start.1 = (bf16[128,40,128]{2,0,1:T(8,128)(2,1)}, bf16[128,40,128]{2,0,1:T(8,128)(2,1)}, u32[]{:S(2)}, u32[]{:S(2)}) collective-permute-start(bf16[128,40,128]{2,0,1:T(8,128)(2,1)} %get-tuple-element.298), channel_id=1, source_target_pairs={{0,1},{1,2},{2,3},{3,4},{4,5},{5,6},{6,7},{7,8},{8,9},{9,10},{10,1... | collective-permute-start | bytes 3932168 | tf_op jit(solution)/shard_map/while/body/eval_jaxpr/ppermute | solution.py:83
  1638.4 34.2 %collective-permute-start.1 = (bf16[128,40,128]{2,0,1:T(8,128)(2,1)}, bf16[128,40,128]{2,0,1:T(8,128)(2,1)}, u32[]{:S(2)}, u32[]{:S(2)}) collective-permute-start(bf16[128,40,128]{2,0,1:T(8,128)(2,1)} %get-tuple-element.298), channel_id=1, source_target_pairs={{0,1},{1,2},{2,3},{3,4},{4,5},{5,6},{6,7},{7,8},{8,9},{9,10},{10,1... | collective-permute-start | bytes 3932168 | tf_op jit(solution)/shard_map/while/body/eval_jaxpr/ppermute | solution.py:83
  1681.6 31.5 %collective-permute-start = (bf16[128,40,128]{2,0,1:T(8,128)(2,1)}, bf16[128,40,128]{2,0,1:T(8,128)(2,1)S(1)}, u32[]{:S(2)}, u32[]{:S(2)}) collective-permute-start(bf16[128,40,128]{2,0,1:T(8,128)(2,1)} %get-tuple-element.297), channel_id=1, source_target_pairs={{0,1},{1,2},{2,3},{3,4},{4,5},{5,6},{6,7},{7,8},{8,9},{9,10},{10,1... | collective-permute-start | bytes 3932168 | tf_op jit(solution)/shard_map/while/body/eval_jaxpr/ppermute | solution.py:82
  1681.6 34.2 %collective-permute-start.1 = (bf16[128,40,128]{2,0,1:T(8,128)(2,1)}, bf16[128,40,128]{2,0,1:T(8,128)(2,1)}, u32[]{:S(2)}, u32[]{:S(2)}) collective-permute-start(bf16[128,40,128]{2,0,1:T(8,128)(2,1)} %get-tuple-element.298), channel_id=1, source_target_pairs={{0,1},{1,2},{2,3},{3,4},{4,5},{5,6},{6,7},{7,8},{8,9},{9,10},{10,1... | collective-permute-start | bytes 3932168 | tf_op jit(solution)/shard_map/while/body/eval_jaxpr/ppermute | solution.py:83
  1724.9 34.2 %collective-permute-start.1 = (bf16[128,40,128]{2,0,1:T(8,128)(2,1)}, bf16[128,40,128]{2,0,1:T(8,128)(2,1)}, u32[]{:S(2)}, u32[]{:S(2)}) collective-permute-start(bf16[128,40,128]{2,0,1:T(8,128)(2,1)} %get-tuple-element.298), channel_id=1, source_target_pairs={{0,1},{1,2},{2,3},{3,4},{4,5},{5,6},{6,7},{7,8},{8,9},{9,10},{10,1... | collective-permute-start | bytes 3932168 | tf_op jit(solution)/shard_map/while/body/eval_jaxpr/ppermute | solution.py:83
  1768.1 34.2 %collective-permute-start.1 = (bf16[128,40,128]{2,0,1:T(8,128)(2,1)}, bf16[128,40,128]{2,0,1:T(8,128)(2,1)}, u32[]{:S(2)}, u32[]{:S(2)}) collective-permute-start(bf16[128,40,128]{2,0,1:T(8,128)(2,1)} %get-tuple-element.298), channel_id=1, source_target_pairs={{0,1},{1,2},{2,3},{3,4},{4,5},{5,6},{6,7},{7,8},{8,9},{9,10},{10,1... | collective-permute-start | bytes 3932168 | tf_op jit(solution)/shard_map/while/body/eval_jaxpr/ppermute | solution.py:83
  1811.4 34.2 %collective-permute-start.1 = (bf16[128,40,128]{2,0,1:T(8,128)(2,1)}, bf16[128,40,128]{2,0,1:T(8,128)(2,1)}, u32[]{:S(2)}, u32[]{:S(2)}) collective-permute-start(bf16[128,40,128]{2,0,1:T(8,128)(2,1)} %get-tuple-element.298), channel_id=1, source_target_pairs={{0,1},{1,2},{2,3},{3,4},{4,5},{5,6},{6,7},{7,8},{8,9},{9,10},{10,1... | collective-permute-start | bytes 3932168 | tf_op jit(solution)/shard_map/while/body/eval_jaxpr/ppermute | solution.py:83
  1854.6 31.5 %collective-permute-start = (bf16[128,40,128]{2,0,1:T(8,128)(2,1)}, bf16[128,40,128]{2,0,1:T(8,128)(2,1)S(1)}, u32[]{:S(2)}, u32[]{:S(2)}) collective-permute-start(bf16[128,40,128]{2,0,1:T(8,128)(2,1)} %get-tuple-element.297), channel_id=1, source_target_pairs={{0,1},{1,2},{2,3},{3,4},{4,5},{5,6},{6,7},{7,8},{8,9},{9,10},{10,1... | collective-permute-start | bytes 3932168 | tf_op jit(solution)/shard_map/while/body/eval_jaxpr/ppermute | solution.py:82
  1854.6 34.2 %collective-permute-start.1 = (bf16[128,40,128]{2,0,1:T(8,128)(2,1)}, bf16[128,40,128]{2,0,1:T(8,128)(2,1)}, u32[]{:S(2)}, u32[]{:S(2)}) collective-permute-start(bf16[128,40,128]{2,0,1:T(8,128)(2,1)} %get-tuple-element.298), channel_id=1, source_target_pairs={{0,1},{1,2},{2,3},{3,4},{4,5},{5,6},{6,7},{7,8},{8,9},{9,10},{10,1... | collective-permute-start | bytes 3932168 | tf_op jit(solution)/shard_map/while/body/eval_jaxpr/ppermute | solution.py:83
  1897.9 34.2 %collective-permute-start.1 = (bf16[128,40,128]{2,0,1:T(8,128)(2,1)}, bf16[128,40,128]{2,0,1:T(8,128)(2,1)}, u32[]{:S(2)}, u32[]{:S(2)}) collective-permute-start(bf16[128,40,128]{2,0,1:T(8,128)(2,1)} %get-tuple-element.298), channel_id=1, source_target_pairs={{0,1},{1,2},{2,3},{3,4},{4,5},{5,6},{6,7},{7,8},{8,9},{9,10},{10,1... | collective-permute-start | bytes 3932168 | tf_op jit(solution)/shard_map/while/body/eval_jaxpr/ppermute | solution.py:83
  (86 other events, 692.6 us)
Sparse Core Ops, SparseCore 0:
  30.7 134.6 all-gather.2
  168.0 129.4 all-gather.4
where the time goes:
time: 2000 us; the launch traced here: 1970 us
  waiting for transfers between devices  1430 us (72%)
  matrix products  276 us (14%)
  local copies, waits for them, and re-layouts  179 us (9%)
  starting transfers between devices  45.8 us (2%)
  other arithmetic  25.7 us (1%)
    ppermute x31, waiting for transfers between devices, cache_step(): k_blk = lax.ppermute(k_blk, SEQ_AXES, perm_next)  1210 us
    while x186, local copies, waits for them, and re-layouts  164 us
    dot_general x34, matrix products, attend_block(): jnp.einsum('hgqk,khd->hgqd', exp_scores.astype(jnp.bfloat16), values, pre...  163 us
    all_gather x1, waiting for transfers between devices, local_fn(): v_fresh = lax.all_gather(v_new, SEQ_AXES, axis=0, tiled=True)  132 us
    all_gather x1, waiting for transfers between devices, local_fn(): k_fresh = lax.all_gather(k_new, SEQ_AXES, axis=0, tiled=True)  77 us
  transfers between devices with their start and end apart: 64, of which 34 were waited for; matrix products, arithmetic and copies ran while one was open for 7% of the time, Pallas kernels for 0%

commit v1 on v0

v1 whole, which is shorter than its diff:
```python
import functools
import math

import jax
import jax.numpy as jnp
from jax import lax
from jax.experimental import pallas as pl
from jax.experimental.pallas import tpu as pltpu
from jax.sharding import PartitionSpec as P

ROPE_BASE = 500000
MESH = pl.DeviceIdType.MESH
COLS = 512
NBUF = 4
QB = 512
QC = QB // 2
KB = 1024


def rope_tables(positions, head_dim):
    inv_freq = 1.0 / (ROPE_BASE ** (jnp.arange(0, head_dim, 2, dtype=jnp.float32) / head_dim))
    angles = positions.astype(jnp.float32)[:, None] * inv_freq[None, :]
    cos_t, sin_t = jnp.cos(angles), jnp.sin(angles)
    return jnp.concatenate([cos_t, cos_t], axis=-1), jnp.concatenate([-sin_t, sin_t], axis=-1)


def online_step(q, k, v, m, l, acc, coef, mask=None):
    s = lax.dot_general(q, k, (((1,), (1,)), ((), ())), preferred_element_type=jnp.float32)
    if mask is not None:
        s = jnp.where(mask, s, -jnp.inf)
    m_new = jnp.maximum(m, jnp.max(s, axis=1, keepdims=True))
    p = jnp.exp2((s - m_new) * coef)
    alpha = jnp.exp2((m - m_new) * coef)
    part = p[:, :128]
    for lane in range(128, p.shape[1], 128):
        part = part + p[:, lane:lane + 128]
    pv = jnp.dot(p.astype(jnp.bfloat16), v, preferred_element_type=jnp.float32)
    return m_new, l * alpha + part, acc * alpha + pv


def kernel(sp, cp, heads, head_dim,
           x_ref, cos_ref, sin_ref, kc_hbm, vc_hbm, wq_hbm, wk_hbm, wv_hbm, wo_hbm,
           y_ref, kn_ref, vn_ref,
           q_loc, q_all, kc_all, vc_all, kn_all, vn_all, o_all, o_loc,
           m_st, l_st, acc_st, wbuf, wsem, ssem, rsem):
    S = sp * cp
    E = heads - S
    G = S // E
    t = x_ref.shape[0]
    d_model = x_ref.shape[1]
    L = S * t
    me = lax.axis_index('sp') * cp + lax.axis_index('cp')
    per = S // (2 * G)
    rank = lax.rem(me, G)
    xhead = S + lax.div(me, G)
    my_blk = lax.div(me, per)
    my_rank = jnp.minimum(my_blk, 2 * G - 1 - my_blk)
    hi_share = my_blk >= G
    own_extra = my_rank == rank
    coef = (head_dim ** -0.5) * math.log2(math.e)

    def dev(idx):
        return {'sp': lax.div(idx, cp), 'cp': lax.rem(idx, cp)}

    def col(h):
        return pl.ds(pl.multiple_of(h * head_dim, head_dim), head_dim)

    def rows(start, size):
        return pl.ds(pl.multiple_of(start, 128), size)

    def send(src, dst, sem, tgt):
        pltpu.make_async_remote_copy(src_ref=src, dst_ref=dst, send_sem=ssem.at[sem], recv_sem=rsem.at[sem],
                                     device_id=dev(tgt), device_id_type=MESH).start()

    def local(src, dst, sem):
        pltpu.make_async_copy(src, dst, rsem.at[sem]).start()

    def wait_recv(buf, sem):
        pltpu.make_async_copy(buf, buf, rsem.at[sem]).wait()

    def wait_sent(buf, n_pieces, sem):
        part = buf.at[pl.ds(0, n_pieces * t)]
        pltpu.make_async_copy(part, part, ssem.at[sem]).wait()

    tiles = d_model // COLS
    weights = (wq_hbm, wk_hbm, wv_hbm, wo_hbm)

    def fetch(w, tile, slot):
        return pltpu.make_async_copy(w.at[:, pl.ds(pl.multiple_of(tile * COLS, COLS), COLS)], wbuf.at[slot], wsem.at[slot])

    for tile in range(NBUF - 1):
        fetch(wq_hbm, tile, tile).start()

    barrier = pltpu.get_barrier_semaphore()

    def greet(d, carry):
        pl.semaphore_signal(barrier, inc=1, device_id=dev(lax.rem(me + d, S)), device_id_type=MESH)
        return carry

    lax.fori_loop(1, S, greet, 0)
    pl.semaphore_wait(barrier, S - 1)

    def send_kv(src, dst, sem):
        local(src.at[:, col(me)], dst.at[rows(me * t, t)], sem)
        local(src.at[:, col(xhead)], dst.at[rows(L + me * t, t)], sem)

    def send_pair(pair):
        for src, dst, sem in pair:
            send_kv(src, dst, sem)

        def to_peer(d, carry):
            tgt = lax.rem(me + d, S)
            for src, dst, sem in pair:
                send(src.at[:, col(tgt)], dst.at[rows(me * t, t)], sem, tgt)
                send(src.at[:, col(S + lax.div(tgt, G))], dst.at[rows(L + me * t, t)], sem, tgt)
            return carry

        lax.fori_loop(1, S, to_peer, 0)

    send_pair(((kc_hbm, kc_all, 0), (vc_hbm, vc_all, 1)))

    def project(which, out_fn, first_tile, next_w):
        def body(i, carry):
            step = which * tiles + i
            slot = lax.rem(step, NBUF)
            fetch(weights[which], i, slot).wait()
            acc = jnp.dot(out_fn[0][...], wbuf[slot], preferred_element_type=jnp.float32).astype(jnp.bfloat16)
            ahead = i + NBUF - 1
            nslot = lax.rem(step + NBUF - 1, NBUF)

            @pl.when(ahead < tiles)
            def _():
                fetch(weights[which], ahead, nslot).start()

            if next_w is not None:
                @pl.when(ahead >= tiles)
                def _():
                    fetch(next_w, ahead - tiles, nslot).start()

            out_fn[1](i, acc)
            return carry

        lax.fori_loop(first_tile, tiles, body, 0)

    def store_rope(dst):
        def put(i, val):
            for h in range(COLS // head_dim):
                piece = val[:, h * head_dim:(h + 1) * head_dim].astype(jnp.float32)
                turned = piece * cos_ref[...] + pltpu.roll(piece, head_dim // 2, 1) * sin_ref[...]
                dst[:, pl.ds(pl.multiple_of(i * COLS + h * head_dim, head_dim), head_dim)] = turned.astype(jnp.bfloat16)
        return put

    def store_plain(dst):
        def put(i, val):
            dst[:, pl.ds(pl.multiple_of(i * COLS, COLS), COLS)] = val
        return put

    project(0, (x_ref, store_rope(q_loc)), 0, wk_hbm)

    local(q_loc.at[:, col(me)], q_all.at[rows(me * t, t)], 2)

    def q_peer(d, carry):
        tgt = lax.rem(me + d, S)
        send(q_loc.at[:, col(tgt)], q_all.at[rows(me * t, t)], 2, tgt)
        return carry

    lax.fori_loop(1, S, q_peer, 0)
    xrow = L + jnp.where(hi_share, per * t, 0) + lax.rem(me, per) * t

    def q_extra(g, carry):
        tgt = g * G + my_rank

        @pl.when(tgt == me)
        def _():
            local(q_loc.at[:, col(S + g)], q_all.at[rows(xrow, t)], 2)

        @pl.when(tgt != me)
        def _():
            send(q_loc.at[:, col(S + g)], q_all.at[rows(xrow, t)], 2, tgt)
        return carry

    lax.fori_loop(0, E, q_extra, 0)

    project(1, (x_ref, store_rope(kn_ref)), 0, wv_hbm)
    send_pair(((kn_ref, kn_all, 3),))
    project(2, (x_ref, store_plain(vn_ref)), 0, wo_hbm)
    send_pair(((vn_ref, vn_all, 4),))

    nmain = L // QB
    nq = nmain + 2 * per * t // QB

    def block_pos(qb):
        return jnp.where(qb < nmain, qb, jnp.where(qb == nmain, rank, 2 * G - 1 - rank))

    wait_recv(q_all, 2)
    wait_recv(kc_all, 0)
    wait_recv(vc_all, 1)

    def cache_block(qb, carry):
        base = jnp.where(qb < nmain, 0, L)
        qs = [q_all[rows(qb * QB + c * QC, QC), :] for c in range(2)]

        def step(j, state):
            k = kc_all[rows(base + j * KB, KB), :]
            v = vc_all[rows(base + j * KB, KB), :]
            return tuple(online_step(qs[c], k, v, *state[c], coef) for c in range(2))

        init = tuple((jnp.full((QC, 1), -jnp.inf, jnp.float32), jnp.zeros((QC, 128), jnp.float32),
                      jnp.zeros((QC, head_dim), jnp.float32)) for _ in range(2))
        state = lax.fori_loop(0, L // KB, step, init)
        for c in range(2):
            r = rows(qb * QB + c * QC, QC)
            m_st[r, :], l_st[r, :], acc_st[r, :] = state[c]
        return carry

    lax.fori_loop(0, nq, cache_block, 0)

    wait_recv(kn_all, 3)
    wait_recv(vn_all, 4)

    def send_out(qb):
        head = jnp.where(qb < nmain, me, xhead)
        for piece in range(QB // t):
            tgt = block_pos(qb) * (QB // t) + piece
            src = o_all.at[rows(qb * QB + piece * t, t)]
            dst = o_loc.at[:, col(head)]

            @pl.when(tgt == me)
            def _():
                local(src, dst, 5)

            @pl.when(tgt != me)
            def _():
                send(src, dst, 5, tgt)

    def new_block(qb, carry):
        base = jnp.where(qb < nmain, 0, L)
        pos = block_pos(qb)
        r = [rows(qb * QB + c * QC, QC) for c in range(2)]
        qs = [q_all[r[c], :] for c in range(2)]
        init = tuple((m_st[r[c], :], l_st[r[c], :], acc_st[r[c], :]) for c in range(2))

        def step(j, state):
            k = kn_all[rows(base + j * QB, QB), :]
            v = vn_all[rows(base + j * QB, QB), :]
            return tuple(online_step(qs[c], k, v, *state[c], coef) for c in range(2))

        state = lax.fori_loop(0, pos, step, init)
        for c in range(2):
            span = (c + 1) * QC
            k = kn_all[rows(base + pos * QB, span), :]
            v = vn_all[rows(base + pos * QB, span), :]
            mask = (lax.broadcasted_iota(jnp.int32, (QC, span), 1)
                    <= lax.broadcasted_iota(jnp.int32, (QC, span), 0) + c * QC)
            _, l, acc = online_step(qs[c], k, v, *state[c], coef, mask)
            o_all[r[c], :] = (acc / jnp.sum(l, axis=1, keepdims=True)).astype(jnp.bfloat16)

        @pl.when(qb > 0)
        def _():
            send_out(qb - 1)
        return carry

    lax.fori_loop(0, nq, new_block, 0)
    send_out(nq - 1)

    wait_recv(o_loc, 5)
    project(3, (o_loc, store_plain(y_ref)), 0, None)

    for buf, sem in ((kc_all, 0), (vc_all, 1), (kn_all, 3), (vn_all, 4)):
        wait_sent(buf, 2 * (S - 1), sem)
    for sem in (2, 5):
        wait_sent(q_all, S - 1, sem)

        @pl.when(own_extra)
        def _():
            wait_sent(q_all, E - 1, sem)

        @pl.when(jnp.logical_not(own_extra))
        def _():
            wait_sent(q_all, E, sem)


def solution(mesh):
    sp, cp = mesh.shape['sp'], mesh.shape['cp']
    S = sp * cp
    row_spec = P(('dp', 'sp', 'cp'))

    def local_fn(x_loc, kc_loc, vc_loc, w_q, w_k, w_v, w_o):
        t, d_model = x_loc.shape
        _, heads, hd = kc_loc.shape
        G = S // (heads - S)
        L, X = S * t, S * t // G
        width = heads * hd
        seq_idx = lax.axis_index('sp') * cp + lax.axis_index('cp')
        cos_t, sin_t = rope_tables(L + seq_idx * t + jnp.arange(t), hd)
        bf, f32 = jnp.bfloat16, jnp.float32
        vmem, hbm = pl.BlockSpec(memory_space=pltpu.VMEM), pl.BlockSpec(memory_space=pl.ANY)
        y, k_new, v_new = pl.pallas_call(
            functools.partial(kernel, sp, cp, heads, hd),
            out_shape=[jax.ShapeDtypeStruct((t, d_model), bf), jax.ShapeDtypeStruct((t, width), bf),
                       jax.ShapeDtypeStruct((t, width), bf)],
            in_specs=[vmem, vmem, vmem] + [hbm] * 6,
            out_specs=[vmem] * 3,
            scratch_shapes=[
                pltpu.VMEM((t, width), bf),
                pltpu.VMEM((L + X, hd), bf),
                pltpu.VMEM((2 * L, hd), bf), pltpu.VMEM((2 * L, hd), bf),
                pltpu.VMEM((2 * L, hd), bf), pltpu.VMEM((2 * L, hd), bf),
                pltpu.VMEM((L + X, hd), bf),
                pltpu.VMEM((t, width), bf),
                pltpu.VMEM((L + X, 1), f32), pltpu.VMEM((L + X, 128), f32), pltpu.VMEM((L + X, hd), f32),
                pltpu.VMEM((NBUF, d_model, COLS), bf),
                pltpu.SemaphoreType.DMA((NBUF,)),
                pltpu.SemaphoreType.DMA((6,)),
                pltpu.SemaphoreType.DMA((6,)),
            ],
            compiler_params=pltpu.CompilerParams(collective_id=0, has_side_effects=True, vmem_limit_bytes=67043328),
        )(x_loc, cos_t, sin_t, kc_loc.reshape(t, width), vc_loc.reshape(t, width), w_q, w_k, w_v, w_o)
        return y, k_new.reshape(t, heads, hd), v_new.reshape(t, heads, hd)

    return jax.shard_map(local_fn, mesh=mesh, in_specs=(row_spec, row_spec, row_spec, P(), P(), P(), P()), out_specs=(row_spec, row_spec, row_spec), check_vma=False)
```

time: 2000 us -> 247 us (0.12); the launches traced: 1970 us -> 247 us
  waiting for transfers between devices: 1430 us -> 0 us
  matrix products: 276 us -> 0 us
  Pallas kernels: 0 us -> 236 us
  local copies, waits for them, and re-layouts: 179 us -> 9.03 us
  starting transfers between devices: 45.8 us -> 0 us
  other arithmetic: 25.7 us -> 1.08 us
    ppermute x62 -> x0, waiting for transfers between devices: 1220 us -> none  [the longest x31 1210 us: cache_step(): k_blk = lax.ppermute(k_blk, SEQ_AXES, perm_next)]
    dot_general x72 -> x0, matrix products: 276 us -> none  [the longest x34 163 us: attend_block(): jnp.einsum('hgqk,khd->hgqd', exp_scores.astype(jnp.bfloat16), values, pre...]
    pallas_call x0 -> x1, Pallas kernels: none -> 236 us  [local_fn(): pl.pallas_call(functools.partial(kernel, sp, cp, heads, hd), out_shape=[j...]
    all_gather x2 -> x0, waiting for transfers between devices: 209 us -> none  [the longest x1 132 us: local_fn(): v_fresh = lax.all_gather(v_new, SEQ_AXES, axis=0, tiled=True)]
    while x188 -> x0, local copies, waits for them, and re-layouts: 168 us -> none
    ppermute x62 -> x0, starting transfers between devices: 45.5 us -> none  [the longest x31 31 us: cache_step(): v_blk = lax.ppermute(v_blk, SEQ_AXES, perm_next)]
  transfers between devices with their start and end apart: 64 -> 0, of which waited for: 34 -> 0; matrix products, arithmetic and copies ran while one was open for 7% -> 0% of each run, Pallas kernels for 0% -> 0%
where the time goes in v1:
time: 247 us
  Pallas kernels  236 us (96%)
  local copies, waits for them, and re-layouts  9.03 us (4%)
    pallas_call x1, Pallas kernels, local_fn(): pl.pallas_call(functools.partial(kernel, sp, cp, heads, hd), out_shape=[j...  236 us
    unnamed x7, local copies, waits for them, and re-layouts  5.42 us

profile of v1, /device:TPU:97, one launch (start us, length us, event | category | flops | bytes accessed | tf_op | source)
XLA Modules:
  0.0 247.0 jit_solution(17651140508463438647)
XLA Ops:
  0.7 0.3 fusion
  1.0 0.8 pad_maximum_fusion
  1.7 3.6 %copy_bitcast_fusion = (bf16[128,5120]{1,0:T(8,128)(2,1)}, bf16[128,5120]{1,0:T(8,128)(2,1)}) fusion(bf16[16,8,40,128]{3,2,1,0:T(8,128)(2,1)} %bitcast.10, bf16[16,8,40,128]{3,2,1,0:T(8,128)(2,1)} %bitcast.11), kind=kLoop, calls=%fused_computation | loop fusion | bytes 5242880 | tf_op jit(solution)/shard_map/reshape | solution.py:318
  5.3 236.2 %shard_map.94 = (bf16[128,5120]{1,0:T(8,128)(2,1)}, bf16[128,5120]{1,0:T(8,128)(2,1)}, bf16[128,5120]{1,0:T(8,128)(2,1)}) custom-call(bf16[128,5120]{1,0:T(8,128)(2,1)} %x_ref.1, f32[128,128]{1,0:T(8,128)} %get-tuple-element.12.cos_ref, f32[128,128]{1,0:T(8,128)} %get-tuple-element.13.sin_ref, bf16[128,5120]{1,0:T(8,128)(2,1)} %get-tuple-element.15.kc_hbm, ...), custom_call_target="tpu_custom_call" | custom-call | tf_op jit(solution)/shard_map/pallas_call | solution.py:298
  241.5 0.0 copy-start.1
  241.5 2.7 %copy.12 = bf16[16,8,40,128]{3,2,1,0:T(8,128)(2,1)} copy(bf16[16,8,40,128]{3,1,2,0:T(8,128)(2,1)} %bitcast.15) | data formatting | bytes 2621440
  244.3 0.0 copy-done.1
  244.3 0.0 copy-start
  244.3 1.3 copy.13
  245.6 0.3 copy-done
  245.9 1.1 copy.17
  (2 shorter events, 0.0 us)
Async XLA Ops:
  241.5 2.7 %copy-start.1 = (bf16[128,5120]{1,0:T(8,128)(2,1)S(1)}, bf16[128,5120]{1,0:T(8,128)(2,1)}, u32[]{:S(2)}) copy-start(bf16[128,5120]{1,0:T(8,128)(2,1)} %get-tuple-element.8) | copy-start | bytes 3932164
  244.3 1.6 copy-start

commit v2 on v1

--- a/solution.py
+++ b/solution.py
@@ -13,7 +13,7 @@
 COLS = 512
 NBUF = 4
 QB = 512
-QC = QB // 2
+SUB = 512
 KB = 1024
 
 
@@ -24,25 +24,33 @@
     return jnp.concatenate([cos_t, cos_t], axis=-1), jnp.concatenate([-sin_t, sin_t], axis=-1)
 
 
-def online_step(q, k, v, m, l, acc, coef, mask=None):
-    s = lax.dot_general(q, k, (((1,), (1,)), ((), ())), preferred_element_type=jnp.float32)
+def score_piece(i, q, k_at, s_buf, top, mask):
+    s = lax.dot_general(k_at(i), q, (((1,), (1,)), ((), ())), preferred_element_type=jnp.float32)
     if mask is not None:
-        s = jnp.where(mask, s, -jnp.inf)
-    m_new = jnp.maximum(m, jnp.max(s, axis=1, keepdims=True))
-    p = jnp.exp2((s - m_new) * coef)
+        s = jnp.where(mask(i), s, -jnp.inf)
+    s_buf[i * SUB:(i + 1) * SUB, :] = s
+    return jnp.maximum(top, jnp.max(s, axis=0, keepdims=True))
+
+
+def online_step(s_buf, top, v_at, state, coef, pieces, ahead):
+    m, l, acc = state
+    m_new = jnp.maximum(m, top)
     alpha = jnp.exp2((m - m_new) * coef)
-    part = p[:, :128]
-    for lane in range(128, p.shape[1], 128):
-        part = part + p[:, lane:lane + 128]
-    pv = jnp.dot(p.astype(jnp.bfloat16), v, preferred_element_type=jnp.float32)
-    return m_new, l * alpha + part, acc * alpha + pv
+    l, acc = l * alpha, acc * alpha
+    top_next = jnp.full_like(m, -jnp.inf)
+    for i in range(pieces):
+        top_next = score_piece(i, *ahead[:3], top_next, ahead[3])
+        p = jnp.exp2((s_buf[i * SUB:(i + 1) * SUB, :] - m_new) * coef)
+        l = l + jnp.sum(p.reshape(-1, 8, p.shape[1]), axis=0)
+        acc = acc + jnp.dot(v_at(i), p.astype(jnp.bfloat16), preferred_element_type=jnp.float32)
+    return (m_new, l, acc), top_next
 
 
 def kernel(sp, cp, heads, head_dim,
            x_ref, cos_ref, sin_ref, kc_hbm, vc_hbm, wq_hbm, wk_hbm, wv_hbm, wo_hbm,
            y_ref, kn_ref, vn_ref,
-           q_loc, q_all, kc_all, vc_all, kn_all, vn_all, o_all, o_loc,
-           m_st, l_st, acc_st, wbuf, wsem, ssem, rsem):
+           q_loc, vt_loc, q_all, kc_all, vc_all, kn_all, vn_all, o_all, o_loc,
+           m_st, l_st, acc_st, s_a, s_b, s_c, wbuf, wsem, ssem, rsem):
     S = sp * cp
     E = heads - S
     G = S // E
@@ -59,6 +67,15 @@
     own_extra = my_rank == rank
     coef = (head_dim ** -0.5) * math.log2(math.e)
 
+    X = cp // 2
+    my_y, my_x, my_core = lax.div(me, cp), lax.div(lax.rem(me, cp), 2), lax.rem(me, 2)
+
+    def peer(d):
+        core, chip = lax.div(d, S // 2), lax.rem(d, S // 2)
+        dx = lax.rem(chip, X)
+        dy = lax.rem(lax.div(chip, X) + dx, sp)
+        return lax.rem(my_y + dy, sp) * cp + lax.rem(my_x + dx, X) * 2 + lax.rem(my_core + core, 2)
+
     def dev(idx):
         return {'sp': lax.div(idx, cp), 'cp': lax.rem(idx, cp)}
 
@@ -100,24 +117,30 @@
     lax.fori_loop(1, S, greet, 0)
     pl.semaphore_wait(barrier, S - 1)
 
-    def send_kv(src, dst, sem):
-        local(src.at[:, col(me)], dst.at[rows(me * t, t)], sem)
-        local(src.at[:, col(xhead)], dst.at[rows(L + me * t, t)], sem)
-
-    def send_pair(pair):
-        for src, dst, sem in pair:
-            send_kv(src, dst, sem)
-
-        def to_peer(d, carry):
-            tgt = lax.rem(me + d, S)
-            for src, dst, sem in pair:
-                send(src.at[:, col(tgt)], dst.at[rows(me * t, t)], sem, tgt)
-                send(src.at[:, col(S + lax.div(tgt, G))], dst.at[rows(L + me * t, t)], sem, tgt)
-            return carry
-
-        lax.fori_loop(1, S, to_peer, 0)
-
-    send_pair(((kc_hbm, kc_all, 0), (vc_hbm, vc_all, 1)))
+    def head_of(sel, idx):
+        return idx if sel == 0 else S + lax.div(idx, G)
+
+    def k_piece(src, dst, sel, idx):
+        return src.at[:, col(head_of(sel, idx))], dst.at[rows(sel * L + me * t, t)]
+
+    def v_piece(src, dst, sel, idx):
+        return (src.at[rows(head_of(sel, idx) * head_dim, head_dim)],
+                dst.at[pl.ds(sel * head_dim, head_dim), rows(me * t, t)])
+
+    def send_all(groups):
+        for piece, src, dst, sem in groups:
+            for sel in range(2):
+                local(*piece(src, dst, sel, me), sem)
+        for piece, src, dst, sem in groups:
+            for sel in range(2):
+                def to_peer(d, carry, piece=piece, src=src, dst=dst, sem=sem, sel=sel):
+                    tgt = peer(d)
+                    send(*piece(src, dst, sel, tgt), sem, tgt)
+                    return carry
+
+                lax.fori_loop(1, S, to_peer, 0)
+
+    send_all(((k_piece, kc_hbm, kc_all, 0), (v_piece, vc_hbm, vc_all, 1)))
 
     def project(which, out_fn, first_tile, next_w):
         def body(i, carry):
@@ -155,12 +178,16 @@
             dst[:, pl.ds(pl.multiple_of(i * COLS, COLS), COLS)] = val
         return put
 
+    def store_values(i, val):
+        vn_ref[:, pl.ds(pl.multiple_of(i * COLS, COLS), COLS)] = val
+        vt_loc[pl.ds(pl.multiple_of(i * COLS, COLS), COLS), :] = val.T
+
     project(0, (x_ref, store_rope(q_loc)), 0, wk_hbm)
 
     local(q_loc.at[:, col(me)], q_all.at[rows(me * t, t)], 2)
 
     def q_peer(d, carry):
-        tgt = lax.rem(me + d, S)
+        tgt = peer(d)
         send(q_loc.at[:, col(tgt)], q_all.at[rows(me * t, t)], 2, tgt)
         return carry
 
@@ -182,9 +209,9 @@
     lax.fori_loop(0, E, q_extra, 0)
 
     project(1, (x_ref, store_rope(kn_ref)), 0, wv_hbm)
-    send_pair(((kn_ref, kn_all, 3),))
-    project(2, (x_ref, store_plain(vn_ref)), 0, wo_hbm)
-    send_pair(((vn_ref, vn_all, 4),))
+    send_all(((k_piece, kn_ref, kn_all, 3),))
+    project(2, (x_ref, store_values), 0, wo_hbm)
+    send_all(((v_piece, vt_loc, vn_all, 4),))
 
     nmain = L // QB
     nq = nmain + 2 * per * t // QB
@@ -196,24 +223,40 @@
     wait_recv(kc_all, 0)
     wait_recv(vc_all, 1)
 
-    def cache_block(qb, carry):
-        base = jnp.where(qb < nmain, 0, L)
-        qs = [q_all[rows(qb * QB + c * QC, QC), :] for c in range(2)]
-
-        def step(j, state):
-            k = kc_all[rows(base + j * KB, KB), :]
-            v = vc_all[rows(base + j * KB, KB), :]
-            return tuple(online_step(qs[c], k, v, *state[c], coef) for c in range(2))
-
-        init = tuple((jnp.full((QC, 1), -jnp.inf, jnp.float32), jnp.zeros((QC, 128), jnp.float32),
-                      jnp.zeros((QC, head_dim), jnp.float32)) for _ in range(2))
-        state = lax.fori_loop(0, L // KB, step, init)
-        for c in range(2):
-            r = rows(qb * QB + c * QC, QC)
-            m_st[r, :], l_st[r, :], acc_st[r, :] = state[c]
-        return carry
-
-    lax.fori_loop(0, nq, cache_block, 0)
+    bufs = (s_a, s_b, s_c)
+
+    def k_rows(buf, sel, start):
+        return lambda i: buf[rows(sel * L + start + i * SUB, SUB), :]
+
+    def v_cols(buf, sel, start):
+        return lambda i: buf[rows(sel * head_dim, head_dim), rows(start + i * SUB, SUB)]
+
+    def first_scores(q, k_at, s_buf, pieces):
+        top = jnp.full((1, QB), -jnp.inf, jnp.float32)
+        for i in range(pieces):
+            top = score_piece(i, q, k_at, s_buf, top, None)
+        return top
+
+    def query(qb):
+        return q_all[rows(qb * QB, QB), :]
+
+    nst = L // KB
+
+    def cache_block(qb, top):
+        sel, after = lax.div(qb, nmain), jnp.minimum(qb + 1, nq - 1)
+        q, q_after = query(qb), query(after)
+        state = (jnp.full((1, QB), -jnp.inf, jnp.float32), jnp.zeros((8, QB), jnp.float32),
+                 jnp.zeros((head_dim, QB), jnp.float32))
+        for j in range(nst):
+            if j + 1 < nst:
+                ahead = (q, k_rows(kc_all, sel, (j + 1) * KB), bufs[(j + 1) % 2], None)
+            else:
+                ahead = (q_after, k_rows(kc_all, lax.div(after, nmain), 0), bufs[0], None)
+            state, top = online_step(bufs[j % 2], top, v_cols(vc_all, sel, j * KB), state, coef, KB // SUB, ahead)
+        m_st[qb, 0:1, :], l_st[qb], acc_st[qb] = state
+        return top
+
+    lax.fori_loop(0, nq, cache_block, first_scores(query(0), k_rows(kc_all, 0, 0), s_a, KB // SUB))
 
     wait_recv(kn_all, 3)
     wait_recv(vn_all, 4)
@@ -233,41 +276,51 @@
             def _():
                 send(src, dst, 5, tgt)
 
-    def new_block(qb, carry):
-        base = jnp.where(qb < nmain, 0, L)
-        pos = block_pos(qb)
-        r = [rows(qb * QB + c * QC, QC) for c in range(2)]
-        qs = [q_all[r[c], :] for c in range(2)]
-        init = tuple((m_st[r[c], :], l_st[r[c], :], acc_st[r[c], :]) for c in range(2))
-
-        def step(j, state):
-            k = kn_all[rows(base + j * QB, QB), :]
-            v = vn_all[rows(base + j * QB, QB), :]
-            return tuple(online_step(qs[c], k, v, *state[c], coef) for c in range(2))
-
-        state = lax.fori_loop(0, pos, step, init)
-        for c in range(2):
-            span = (c + 1) * QC
-            k = kn_all[rows(base + pos * QB, span), :]
-            v = vn_all[rows(base + pos * QB, span), :]
-            mask = (lax.broadcasted_iota(jnp.int32, (QC, span), 1)
-                    <= lax.broadcasted_iota(jnp.int32, (QC, span), 0) + c * QC)
-            _, l, acc = online_step(qs[c], k, v, *state[c], coef, mask)
-            o_all[r[c], :] = (acc / jnp.sum(l, axis=1, keepdims=True)).astype(jnp.bfloat16)
-
-        @pl.when(qb > 0)
-        def _():
-            send_out(qb - 1)
-        return carry
-
-    lax.fori_loop(0, nq, new_block, 0)
-    send_out(nq - 1)
+    nfull = nmain - 1
+
+    def item(i, n):
+        qa = jnp.where(i < nmain // 2, i, nmain)
+        qb = jnp.where(i < nmain // 2, nmain - 1 - i, nmain + 1)
+        pa, pb = block_pos(qa), block_pos(qb)
+        if n < nfull:
+            early = n < pa
+            return jnp.where(early, qa, qb), jnp.where(early, n, n - pa), None
+        blk, pos = (qa, pa) if n == nfull else (qb, pb)
+        return blk, pos, lambda piece: (lax.broadcasted_iota(jnp.int32, (SUB, QB), 0) + piece * SUB
+                                        <= lax.broadcasted_iota(jnp.int32, (SUB, QB), 1))
+
+    def new_pair(i, top):
+        after = jnp.minimum(i + 1, nq // 2 - 1)
+        for n in range(nfull + 2):
+            blk, pos, _ = item(i, n)
+            nblk, npos, nmask = item(i, n + 1) if n + 1 < nfull + 2 else item(after, 0)
+            ahead = (query(nblk), k_rows(kn_all, lax.div(nblk, nmain), npos * QB), bufs[(n + 1) % 3], nmask)
+            state = (m_st[blk, 0:1, :], l_st[blk], acc_st[blk])
+            state, top = online_step(bufs[n % 3], top, v_cols(vn_all, lax.div(blk, nmain), pos * QB), state, coef,
+                                     QB // SUB, ahead)
+            if n < nfull:
+                m_st[blk, 0:1, :], l_st[blk], acc_st[blk] = state
+            else:
+                out = (state[2] / jnp.sum(state[1], axis=0, keepdims=True)).astype(jnp.bfloat16)
+                o_all[rows(blk * QB, QB), :] = out.T
+
+        @pl.when(i > 0)
+        def _():
+            send_out(item(i - 1, nfull)[0])
+            send_out(item(i - 1, nfull + 1)[0])
+        return top
+
+    blk0, pos0, _ = item(0, 0)
+    lax.fori_loop(0, nq // 2, new_pair,
+                  first_scores(query(blk0), k_rows(kn_all, lax.div(blk0, nmain), pos0 * QB), s_a, QB // SUB))
+    send_out(item(nq // 2 - 1, nfull)[0])
+    send_out(item(nq // 2 - 1, nfull + 1)[0])
 
     wait_recv(o_loc, 5)
     project(3, (o_loc, store_plain(y_ref)), 0, None)
 
-    for buf, sem in ((kc_all, 0), (vc_all, 1), (kn_all, 3), (vn_all, 4)):
-        wait_sent(buf, 2 * (S - 1), sem)
+    for sem in (0, 1, 3, 4):
+        wait_sent(kc_all, 2 * (S - 1), sem)
     for sem in (2, 5):
         wait_sent(q_all, S - 1, sem)
 
@@ -291,6 +344,7 @@
         G = S // (heads - S)
         L, X = S * t, S * t // G
         width = heads * hd
+        chains = (L + X) // QB
         seq_idx = lax.axis_index('sp') * cp + lax.axis_index('cp')
         cos_t, sin_t = rope_tables(L + seq_idx * t + jnp.arange(t), hd)
         bf, f32 = jnp.bfloat16, jnp.float32
@@ -302,20 +356,21 @@
             in_specs=[vmem, vmem, vmem] + [hbm] * 6,
             out_specs=[vmem] * 3,
             scratch_shapes=[
-                pltpu.VMEM((t, width), bf),
+                pltpu.VMEM((t, width), bf), pltpu.VMEM((width, t), bf),
                 pltpu.VMEM((L + X, hd), bf),
-                pltpu.VMEM((2 * L, hd), bf), pltpu.VMEM((2 * L, hd), bf),
-                pltpu.VMEM((2 * L, hd), bf), pltpu.VMEM((2 * L, hd), bf),
+                pltpu.VMEM((2 * L, hd), bf), pltpu.VMEM((2 * hd, L), bf),
+                pltpu.VMEM((2 * L, hd), bf), pltpu.VMEM((2 * hd, L), bf),
                 pltpu.VMEM((L + X, hd), bf),
                 pltpu.VMEM((t, width), bf),
-                pltpu.VMEM((L + X, 1), f32), pltpu.VMEM((L + X, 128), f32), pltpu.VMEM((L + X, hd), f32),
+                pltpu.VMEM((chains, 8, QB), f32), pltpu.VMEM((chains, 8, QB), f32), pltpu.VMEM((chains, hd, QB), f32),
+                pltpu.VMEM((KB, QB), f32), pltpu.VMEM((KB, QB), f32), pltpu.VMEM((QB, QB), f32),
                 pltpu.VMEM((NBUF, d_model, COLS), bf),
                 pltpu.SemaphoreType.DMA((NBUF,)),
                 pltpu.SemaphoreType.DMA((6,)),
                 pltpu.SemaphoreType.DMA((6,)),
             ],
             compiler_params=pltpu.CompilerParams(collective_id=0, has_side_effects=True, vmem_limit_bytes=67043328),
-        )(x_loc, cos_t, sin_t, kc_loc.reshape(t, width), vc_loc.reshape(t, width), w_q, w_k, w_v, w_o)
+        )(x_loc, cos_t, sin_t, kc_loc.reshape(t, width), vc_loc.transpose(1, 2, 0).reshape(width, t), w_q, w_k, w_v, w_o)
         return y, k_new.reshape(t, heads, hd), v_new.reshape(t, heads, hd)
 
     return jax.shard_map(local_fn, mesh=mesh, in_specs=(row_spec, row_spec, row_spec, P(), P(), P(), P()), out_specs=(row_spec, row_spec, row_spec), check_vma=False)

time: 247 us -> 184 us (0.74)
  Pallas kernels: 236 us -> 172 us
    pallas_call x1, Pallas kernels: 236 us -> 172 us  [local_fn(): pl.pallas_call(functools.partial(kernel, sp, cp, heads, hd), out_shape=[j...]
    reshape x1 -> x0, local copies, waits for them, and re-layouts: 3.61 us -> none  [local_fn(): vc_loc.reshape(t, width)]
    unnamed x7 -> x10, local copies, waits for them, and re-layouts: 5.42 us -> 8.16 us
where the time goes in v2:
time: 184 us
  Pallas kernels  172 us (93%)
  local copies, waits for them, and re-layouts  10 us (5%)
    pallas_call x1, Pallas kernels, local_fn(): pl.pallas_call(functools.partial(kernel, sp, cp, heads, hd), out_shape=[j...  172 us
    unnamed x10, local copies, waits for them, and re-layouts  8.16 us

profile of v2, /device:TPU:97, one launch (start us, length us, event | category | flops | bytes accessed | tf_op | source)
XLA Modules:
  0.0 184.0 jit_solution(15220682076116367569)
XLA Ops:
  0.7 0.3 fusion
  1.0 0.8 pad_maximum_fusion
  1.7 0.0 copy-start
  1.7 2.7 %copy.15 = bf16[16,8,40,128]{3,1,2,0:T(8,128)(2,1)} copy(bf16[16,8,40,128]{3,2,1,0:T(8,128)(2,1)} %bitcast.12) | data formatting | bytes 2621440
  4.5 0.0 copy-done
  4.5 1.9 %copy.10 = bf16[40,128,128]{2,1,0:T(8,128)(2,1)} copy(bf16[40,128,128]{1,0,2:T(8,128)(2,1)S(1)} %bitcast.13) | data formatting | bytes 2621440 | tf_op jit(solution)/shard_map/transpose | solution.py:373
  6.3 172.3 %shard_map.94 = (bf16[128,5120]{1,0:T(8,128)(2,1)}, bf16[128,5120]{1,0:T(8,128)(2,1)}, bf16[128,5120]{1,0:T(8,128)(2,1)}) custom-call(bf16[128,5120]{1,0:T(8,128)(2,1)} %x_ref.1, f32[128,128]{1,0:T(8,128)} %get-tuple-element.12.cos_ref, f32[128,128]{1,0:T(8,128)} %get-tuple-element.13.sin_ref, bf16[128,5120]{1,0:T(8,128)(2,1)} %bitcast.10, ...), custom_call_target="tpu_custom_call" | custom-call | tf_op jit(solution)/shard_map/pallas_call | solution.py:352
  178.6 0.0 copy-start.2
  178.6 2.7 %copy.12 = bf16[16,8,40,128]{3,2,1,0:T(8,128)(2,1)} copy(bf16[16,8,40,128]{3,1,2,0:T(8,128)(2,1)} %bitcast.17) | data formatting | bytes 2621440
  181.4 0.0 copy-done.2
  181.4 0.0 copy-start.1
  181.4 1.3 copy.13
  182.7 0.3 copy-done.1
  183.0 1.1 copy.17
  (2 shorter events, 0.0 us)
Async XLA Ops:
  1.7 2.7 %copy-start = (bf16[128,40,128]{2,1,0:T(8,128)(2,1)S(1)}, bf16[128,40,128]{2,1,0:T(8,128)(2,1)}, u32[]{:S(2)}) copy-start(bf16[128,40,128]{2,1,0:T(8,128)(2,1)} %param.9) | copy-start | bytes 3932164
  178.6 2.7 %copy-start.2 = (bf16[128,5120]{1,0:T(8,128)(2,1)S(1)}, bf16[128,5120]{1,0:T(8,128)(2,1)}, u32[]{:S(2)}) copy-start(bf16[128,5120]{1,0:T(8,128)(2,1)} %get-tuple-element.8) | copy-start | bytes 3932164
  181.4 1.6 copy-start.1

commit v3 on v2

--- a/solution.py
+++ b/solution.py
@@ -11,7 +11,7 @@
 ROPE_BASE = 500000
 MESH = pl.DeviceIdType.MESH
 COLS = 512
-NBUF = 4
+NBUF = 6
 QB = 512
 SUB = 512
 KB = 1024
@@ -127,20 +127,34 @@
         return (src.at[rows(head_of(sel, idx) * head_dim, head_dim)],
                 dst.at[pl.ds(sel * head_dim, head_dim), rows(me * t, t)])
 
-    def send_all(groups):
-        for piece, src, dst, sem in groups:
-            for sel in range(2):
-                local(*piece(src, dst, sel, me), sem)
-        for piece, src, dst, sem in groups:
-            for sel in range(2):
-                def to_peer(d, carry, piece=piece, src=src, dst=dst, sem=sem, sel=sel):
-                    tgt = peer(d)
-                    send(*piece(src, dst, sel, tgt), sem, tgt)
-                    return carry
-
-                lax.fori_loop(1, S, to_peer, 0)
-
-    send_all(((k_piece, kc_hbm, kc_all, 0), (v_piece, vc_hbm, vc_all, 1)))
+    def send_all(piece, src, dst, sem, sel):
+        local(*piece(src, dst, sel, me), sem)
+
+        def to_peer(d, carry):
+            tgt = peer(d)
+            send(*piece(src, dst, sel, tgt), sem, tgt)
+            return carry
+
+        lax.fori_loop(1, S if sel == 0 else S // 2, to_peer, 0)
+
+    def pass_on(piece, dst, sem):
+        def body(n, carry):
+            region = piece(dst, dst, 1, 2 * n + my_core)
+            send(region, region, sem, me + 1 - 2 * my_core)
+            return carry
+
+        lax.fori_loop(0, S // 2, body, 0)
+
+    def k_region(_, dst, sel, idx):
+        return dst.at[rows(sel * L + idx * t, t)]
+
+    def v_region(_, dst, sel, idx):
+        return dst.at[pl.ds(sel * head_dim, head_dim), rows(idx * t, t)]
+
+    send_all(k_piece, kc_hbm, kc_all, 0, 0)
+    send_all(v_piece, vc_hbm, vc_all, 1, 0)
+    send_all(k_piece, kc_hbm, kc_all, 6, 1)
+    send_all(v_piece, vc_hbm, vc_all, 7, 1)
 
     def project(which, out_fn, first_tile, next_w):
         def body(i, carry):
@@ -209,9 +223,11 @@
     lax.fori_loop(0, E, q_extra, 0)
 
     project(1, (x_ref, store_rope(kn_ref)), 0, wv_hbm)
-    send_all(((k_piece, kn_ref, kn_all, 3),))
+    send_all(k_piece, kn_ref, kn_all, 3, 0)
     project(2, (x_ref, store_values), 0, wo_hbm)
-    send_all(((v_piece, vt_loc, vn_all, 4),))
+    send_all(v_piece, vt_loc, vn_all, 4, 0)
+    send_all(k_piece, kn_ref, kn_all, 8, 1)
+    send_all(v_piece, vt_loc, vn_all, 9, 1)
 
     nmain = L // QB
     nq = nmain + 2 * per * t // QB
@@ -220,8 +236,13 @@
         return jnp.where(qb < nmain, qb, jnp.where(qb == nmain, rank, 2 * G - 1 - rank))
 
     wait_recv(q_all, 2)
-    wait_recv(kc_all, 0)
-    wait_recv(vc_all, 1)
+    main_part, half_part = kc_all.at[pl.ds(0, L)], kc_all.at[pl.ds(0, L // 2)]
+    wait_recv(main_part, 0)
+    wait_recv(main_part, 1)
+    wait_recv(half_part, 6)
+    wait_recv(half_part, 7)
+    pass_on(k_region, kc_all, 10)
+    pass_on(v_region, vc_all, 11)
 
     bufs = (s_a, s_b, s_c)
 
@@ -242,8 +263,8 @@
 
     nst = L // KB
 
-    def cache_block(qb, top):
-        sel, after = lax.div(qb, nmain), jnp.minimum(qb + 1, nq - 1)
+    def cache_block(sel, last, qb, top):
+        after = jnp.minimum(qb + 1, last)
         q, q_after = query(qb), query(after)
         state = (jnp.full((1, QB), -jnp.inf, jnp.float32), jnp.zeros((8, QB), jnp.float32),
                  jnp.zeros((head_dim, QB), jnp.float32))
@@ -251,15 +272,26 @@
             if j + 1 < nst:
                 ahead = (q, k_rows(kc_all, sel, (j + 1) * KB), bufs[(j + 1) % 2], None)
             else:
-                ahead = (q_after, k_rows(kc_all, lax.div(after, nmain), 0), bufs[0], None)
+                ahead = (q_after, k_rows(kc_all, sel, 0), bufs[0], None)
             state, top = online_step(bufs[j % 2], top, v_cols(vc_all, sel, j * KB), state, coef, KB // SUB, ahead)
         m_st[qb, 0:1, :], l_st[qb], acc_st[qb] = state
         return top
 
-    lax.fori_loop(0, nq, cache_block, first_scores(query(0), k_rows(kc_all, 0, 0), s_a, KB // SUB))
-
-    wait_recv(kn_all, 3)
-    wait_recv(vn_all, 4)
+    def cache_part(sel, carry):
+        @pl.when(sel == 1)
+        def _():
+            wait_recv(half_part, 10)
+            wait_recv(half_part, 11)
+
+        start, stop = sel * nmain, jnp.where(sel == 0, nmain, nq)
+        lax.fori_loop(start, stop, functools.partial(cache_block, sel, stop - 1),
+                      first_scores(query(start), k_rows(kc_all, sel, 0), s_a, KB // SUB))
+        return carry
+
+    lax.fori_loop(0, 2, cache_part, 0)
+
+    wait_recv(main_part, 3)
+    wait_recv(main_part, 4)
 
     def send_out(qb):
         head = jnp.where(qb < nmain, me, xhead)
@@ -289,14 +321,14 @@
         return blk, pos, lambda piece: (lax.broadcasted_iota(jnp.int32, (SUB, QB), 0) + piece * SUB
                                         <= lax.broadcasted_iota(jnp.int32, (SUB, QB), 1))
 
-    def new_pair(i, top):
-        after = jnp.minimum(i + 1, nq // 2 - 1)
+    def new_pair(sel, last, i, top):
+        after = jnp.minimum(i + 1, last)
         for n in range(nfull + 2):
             blk, pos, _ = item(i, n)
             nblk, npos, nmask = item(i, n + 1) if n + 1 < nfull + 2 else item(after, 0)
-            ahead = (query(nblk), k_rows(kn_all, lax.div(nblk, nmain), npos * QB), bufs[(n + 1) % 3], nmask)
+            ahead = (query(nblk), k_rows(kn_all, sel, npos * QB), bufs[(n + 1) % 3], nmask)
             state = (m_st[blk, 0:1, :], l_st[blk], acc_st[blk])
-            state, top = online_step(bufs[n % 3], top, v_cols(vn_all, lax.div(blk, nmain), pos * QB), state, coef,
+            state, top = online_step(bufs[n % 3], top, v_cols(vn_all, sel, pos * QB), state, coef,
                                      QB // SUB, ahead)
             if n < nfull:
                 m_st[blk, 0:1, :], l_st[blk], acc_st[blk] = state
@@ -304,23 +336,37 @@
                 out = (state[2] / jnp.sum(state[1], axis=0, keepdims=True)).astype(jnp.bfloat16)
                 o_all[rows(blk * QB, QB), :] = out.T
 
-        @pl.when(i > 0)
-        def _():
-            send_out(item(i - 1, nfull)[0])
-            send_out(item(i - 1, nfull + 1)[0])
+        send_out(item(i, nfull)[0])
+        send_out(item(i, nfull + 1)[0])
         return top
 
-    blk0, pos0, _ = item(0, 0)
-    lax.fori_loop(0, nq // 2, new_pair,
-                  first_scores(query(blk0), k_rows(kn_all, lax.div(blk0, nmain), pos0 * QB), s_a, QB // SUB))
-    send_out(item(nq // 2 - 1, nfull)[0])
-    send_out(item(nq // 2 - 1, nfull + 1)[0])
+    def new_part(sel, carry):
+        @pl.when(sel == 1)
+        def _():
+            wait_recv(half_part, 8)
+            wait_recv(half_part, 9)
+            pass_on(k_region, kn_all, 12)
+            pass_on(v_region, vn_all, 13)
+            wait_recv(half_part, 12)
+            wait_recv(half_part, 13)
+
+        start, stop = sel * (nmain // 2), jnp.where(sel == 0, nmain // 2, nq // 2)
+        blk0, pos0, _ = item(start, 0)
+        lax.fori_loop(start, stop, functools.partial(new_pair, sel, stop - 1),
+                      first_scores(query(blk0), k_rows(kn_all, sel, pos0 * QB), s_a, QB // SUB))
+        return carry
+
+    lax.fori_loop(0, 2, new_part, 0)
 
     wait_recv(o_loc, 5)
     project(3, (o_loc, store_plain(y_ref)), 0, None)
 
     for sem in (0, 1, 3, 4):
-        wait_sent(kc_all, 2 * (S - 1), sem)
+        wait_sent(kc_all, S - 1, sem)
+    for sem in (6, 7, 8, 9):
+        wait_sent(kc_all, S // 2 - 1, sem)
+    for sem in (10, 11, 12, 13):
+        wait_sent(kc_all, S // 2, sem)
     for sem in (2, 5):
         wait_sent(q_all, S - 1, sem)
 
@@ -366,8 +412,8 @@
                 pltpu.VMEM((KB, QB), f32), pltpu.VMEM((KB, QB), f32), pltpu.VMEM((QB, QB), f32),
                 pltpu.VMEM((NBUF, d_model, COLS), bf),
                 pltpu.SemaphoreType.DMA((NBUF,)),
-                pltpu.SemaphoreType.DMA((6,)),
-                pltpu.SemaphoreType.DMA((6,)),
+                pltpu.SemaphoreType.DMA((14,)),
+                pltpu.SemaphoreType.DMA((14,)),
             ],
             compiler_params=pltpu.CompilerParams(collective_id=0, has_side_effects=True, vmem_limit_bytes=67043328),
         )(x_loc, cos_t, sin_t, kc_loc.reshape(t, width), vc_loc.transpose(1, 2, 0).reshape(width, t), w_q, w_k, w_v, w_o)

time: 184 us -> 149 us (0.81)
  Pallas kernels: 172 us -> 137 us
    pallas_call x1, Pallas kernels: 172 us -> 137 us  [local_fn(): pl.pallas_call(functools.partial(kernel, sp, cp, heads, hd), out_shape=[j...]
where the time goes in v3:
time: 149 us
  Pallas kernels  137 us (92%)
  local copies, waits for them, and re-layouts  10 us (7%)
    pallas_call x1, Pallas kernels, local_fn(): pl.pallas_call(functools.partial(kernel, sp, cp, heads, hd), out_shape=[j...  137 us
    unnamed x10, local copies, waits for them, and re-layouts  8.16 us

profile of v3, /device:TPU:97, one launch (start us, length us, event | category | flops | bytes accessed | tf_op | source)
XLA Modules:
  0.0 149.1 jit_solution(10482481189783659976)
XLA Ops:
  0.7 0.3 fusion
  1.0 0.8 pad_maximum_fusion
  1.7 0.0 copy-start
  1.7 2.7 %copy.15 = bf16[16,8,40,128]{3,1,2,0:T(8,128)(2,1)} copy(bf16[16,8,40,128]{3,2,1,0:T(8,128)(2,1)} %bitcast.12) | data formatting | bytes 2621440
  4.5 0.0 copy-done
  4.5 1.9 %copy.10 = bf16[40,128,128]{2,1,0:T(8,128)(2,1)} copy(bf16[40,128,128]{1,0,2:T(8,128)(2,1)S(1)} %bitcast.13) | data formatting | bytes 2621440 | tf_op jit(solution)/shard_map/transpose | solution.py:419
  6.3 137.4 %shard_map.94 = (bf16[128,5120]{1,0:T(8,128)(2,1)}, bf16[128,5120]{1,0:T(8,128)(2,1)}, bf16[128,5120]{1,0:T(8,128)(2,1)}) custom-call(bf16[128,5120]{1,0:T(8,128)(2,1)} %x_ref.1, f32[128,128]{1,0:T(8,128)} %get-tuple-element.12.cos_ref, f32[128,128]{1,0:T(8,128)} %get-tuple-element.13.sin_ref, bf16[128,5120]{1,0:T(8,128)(2,1)} %bitcast.10, ...), custom_call_target="tpu_custom_call" | custom-call | tf_op jit(solution)/shard_map/pallas_call | solution.py:398
  143.7 0.0 copy-start.2
  143.7 2.7 %copy.12 = bf16[16,8,40,128]{3,2,1,0:T(8,128)(2,1)} copy(bf16[16,8,40,128]{3,1,2,0:T(8,128)(2,1)} %bitcast.17) | data formatting | bytes 2621440
  146.5 0.0 copy-done.2
  146.5 0.0 copy-start.1
  146.5 1.3 copy.13
  147.8 0.3 copy-done.1
  148.1 1.1 copy.17
  (2 shorter events, 0.0 us)
Async XLA Ops:
  1.7 2.7 %copy-start = (bf16[128,40,128]{2,1,0:T(8,128)(2,1)S(1)}, bf16[128,40,128]{2,1,0:T(8,128)(2,1)}, u32[]{:S(2)}) copy-start(bf16[128,40,128]{2,1,0:T(8,128)(2,1)} %param.9) | copy-start | bytes 3932164
  143.7 2.7 %copy-start.2 = (bf16[128,5120]{1,0:T(8,128)(2,1)S(1)}, bf16[128,5120]{1,0:T(8,128)(2,1)}, u32[]{:S(2)}) copy-start(bf16[128,5120]{1,0:T(8,128)(2,1)} %get-tuple-element.8) | copy-start | bytes 3932164
  146.5 1.6 %copy-start.1 = (bf16[128,5120]{1,0:T(8,128)(2,1)S(1)}, bf16[128,5120]{1,0:T(8,128)(2,1)}, u32[]{:S(2)}) copy-start(bf16[128,5120]{1,0:T(8,128)(2,1)} %get-tuple-element.17) | copy-start | bytes 3932164

commit v4 on v3

--- a/solution.py
+++ b/solution.py
@@ -323,6 +323,14 @@
 
     def new_pair(sel, last, i, top):
         after = jnp.minimum(i + 1, last)
+
+        @pl.when(i == nmain // 2 - 1)
+        def _():
+            wait_recv(half_part, 8)
+            wait_recv(half_part, 9)
+            pass_on(k_region, kn_all, 12)
+            pass_on(v_region, vn_all, 13)
+
         for n in range(nfull + 2):
             blk, pos, _ = item(i, n)
             nblk, npos, nmask = item(i, n + 1) if n + 1 < nfull + 2 else item(after, 0)
@@ -343,10 +351,6 @@
     def new_part(sel, carry):
         @pl.when(sel == 1)
         def _():
-            wait_recv(half_part, 8)
-            wait_recv(half_part, 9)
-            pass_on(k_region, kn_all, 12)
-            pass_on(v_region, vn_all, 13)
             wait_recv(half_part, 12)
             wait_recv(half_part, 13)
 

time: 149 us -> 147 us (0.987)
  Pallas kernels: 137 us -> 135 us
    pallas_call x1, Pallas kernels: 137 us -> 135 us  [local_fn(): pl.pallas_call(functools.partial(kernel, sp, cp, heads, hd), out_shape=[j...]
where the time goes in v4:
time: 147 us; the launch traced here: 146 us
  Pallas kernels  135 us (92%)
  local copies, waits for them, and re-layouts  10 us (7%)
    pallas_call x1, Pallas kernels, local_fn(): pl.pallas_call(functools.partial(kernel, sp, cp, heads, hd), out_shape=[j...  135 us
    unnamed x10, local copies, waits for them, and re-layouts  8.16 us

profile of v4, /device:TPU:97, one launch (start us, length us, event | category | flops | bytes accessed | tf_op | source)
XLA Modules:
  0.0 146.3 jit_solution(2956090679712839955)
XLA Ops:
  0.7 0.3 fusion
  1.0 0.8 pad_maximum_fusion
  1.7 0.0 copy-start
  1.7 2.7 %copy.15 = bf16[16,8,40,128]{3,1,2,0:T(8,128)(2,1)} copy(bf16[16,8,40,128]{3,2,1,0:T(8,128)(2,1)} %bitcast.12) | data formatting | bytes 2621440
  4.5 0.0 copy-done
  4.5 1.9 %copy.10 = bf16[40,128,128]{2,1,0:T(8,128)(2,1)} copy(bf16[40,128,128]{1,0,2:T(8,128)(2,1)S(1)} %bitcast.13) | data formatting | bytes 2621440 | tf_op jit(solution)/shard_map/transpose | solution.py:423
  6.3 134.5 %shard_map.94 = (bf16[128,5120]{1,0:T(8,128)(2,1)}, bf16[128,5120]{1,0:T(8,128)(2,1)}, bf16[128,5120]{1,0:T(8,128)(2,1)}) custom-call(bf16[128,5120]{1,0:T(8,128)(2,1)} %x_ref.1, f32[128,128]{1,0:T(8,128)} %get-tuple-element.12.cos_ref, f32[128,128]{1,0:T(8,128)} %get-tuple-element.13.sin_ref, bf16[128,5120]{1,0:T(8,128)(2,1)} %bitcast.10, ...), custom_call_target="tpu_custom_call" | custom-call | tf_op jit(solution)/shard_map/pallas_call | solution.py:402
  140.9 0.0 copy-start.2
  140.9 2.7 %copy.12 = bf16[16,8,40,128]{3,2,1,0:T(8,128)(2,1)} copy(bf16[16,8,40,128]{3,1,2,0:T(8,128)(2,1)} %bitcast.17) | data formatting | bytes 2621440
  143.6 0.0 copy-done.2
  143.6 0.0 copy-start.1
  143.6 1.3 copy.13
  144.9 0.3 copy-done.1
  145.3 1.1 copy.17
  (2 shorter events, 0.0 us)
Async XLA Ops:
  1.7 2.7 %copy-start = (bf16[128,40,128]{2,1,0:T(8,128)(2,1)S(1)}, bf16[128,40,128]{2,1,0:T(8,128)(2,1)}, u32[]{:S(2)}) copy-start(bf16[128,40,128]{2,1,0:T(8,128)(2,1)} %param.9) | copy-start | bytes 3932164
  140.9 2.7 %copy-start.2 = (bf16[128,5120]{1,0:T(8,128)(2,1)S(1)}, bf16[128,5120]{1,0:T(8,128)(2,1)}, u32[]{:S(2)}) copy-start(bf16[128,5120]{1,0:T(8,128)(2,1)} %get-tuple-element.8) | copy-start | bytes 3932164
  143.6 1.6 %copy-start.1 = (bf16[128,5120]{1,0:T(8,128)(2,1)S(1)}, bf16[128,5120]{1,0:T(8,128)(2,1)}, u32[]{:S(2)}) copy-start(bf16[128,5120]{1,0:T(8,128)(2,1)} %get-tuple-element.17) | copy-start | bytes 3932164
